TPU v7x, 128 devices: a whole 4x4x4 slice. The times are simulated.
128 devices in a mesh: group: 8 (over x, core), tensor: 16 (over y, z).
Axes of the slice: x: 4, y: 4, z: 4, core: 2. Of those that a mesh axis runs over, the one named last changes fastest.
Arguments:
- hidden: bfloat16 [1024, 8192], P('group'), may hold values from -6 to 6
- norm_gain: bfloat16 [8192], replicated, may hold values from 0.5 to 1.5
- query_matrix: bfloat16 [8192, 8192], P(None, 'tensor'), may hold values from -0.0625 to 0.0625
- output_weight: bfloat16 [8192, 8192], P('tensor'), may hold values from -0.0625 to 0.0625
- kv_pages: bfloat16 [1536, 16, 32, 256], P('group', 'tensor'), may hold values from -400 to 400
- page_order: int32 [8, 192], P('group'), may hold values from 0 to 191, each once within a row
- page_counts: int32 [8, 128], P('group'), may hold values from 1 to 8, 192 in all within a row
- page_trims: int32 [8, 128], P('group'), may hold values from 0 to 31
- adapter_store: bfloat16 [64, 8192, 256], P('group', 'tensor'), may hold values from -0.0625 to 0.0625
- store_route: int32 [64, 1], replicated, may hold values from 0 to 7; in each aligned block of 8 rows (0 to 7, 8 to 15, ...) at most 2 rows name the same one
- store_slot: int32 [64], replicated, may hold values from 0 to 7
Outputs:
- layer_out: bfloat16 [1024, 8192], P('group')
Inputs may be any that keep to these rules, and one draw needn't show every extreme that they name: `store_route`: in each group's block of 8 segments no store group is named more than 2 times. `page_order`: each group's row names each of its 192 pages once. `page_counts`: each group's counts sum to 192.
All inputs are finite; a program needn't handle non-finite values.
Results may differ from a plain program's by a relative error of at most 0.0092.
Values may be sent and summed in bfloat16 or wider, within the bound.
A program may use at most 128 MiB of HBM per device.

v0:
```python
import math

import jax
import jax.numpy as jnp
from jax import lax
from jax.sharding import PartitionSpec as P

KVH = 8
HD = 128
SEG = 16
PAGES_MAX = 8


adapter_scale = 2.0
norm_eps = 1e-05
rope_base = 500000.0


def copy_for_each(value, axis):
    copies = jnp.broadcast_to(value, (lax.axis_size(axis), *value.shape))
    return lax.all_to_all(copies, axis, split_axis=0, concat_axis=0, tiled=True)


def taken_together(value, axis):
    everything = copy_for_each(value, axis)
    return jnp.sum(everything, axis=0)


def partner_2(value, axis, stride):
    return lax.ppermute(value, axis, [(i, i ^ 1 << stride) for i in range(lax.axis_size(axis))])


def split_up(value, dim, peers):
    shape = value.shape
    pieces = value.reshape(*shape[:dim], peers, shape[dim] // peers, *shape[dim + 1 :])
    return jnp.moveaxis(pieces, dim, 0)


def sum_at_owner(value, axis, dim):
    pieces = split_up(value, dim, lax.axis_size(axis))
    arrived = lax.all_to_all(pieces, axis, split_axis=0, concat_axis=0, tiled=True)
    return arrived.astype(jnp.float32).sum(axis=0)


def laid_out(pieces, dim):
    shape = list(pieces.shape[1:])
    shape[dim] *= pieces.shape[0]
    return jnp.moveaxis(pieces, 0, dim).reshape(shape)


def gathered_copies(value, axis, dim):
    return laid_out(copy_for_each(value, axis), dim)


def rotate(queries, positions):
    half_dim = queries.shape[-1] // 2
    frequency = rope_base ** (-(jnp.arange(half_dim).astype(jnp.float32) * 2.0) / queries.shape[-1])
    angles = positions[:, None] * frequency[None, :]
    cosine = jnp.cos(angles)[:, None, :]
    sine_table = jnp.sin(angles)[:, None, :]
    lower_part = queries[..., :half_dim]
    upper_part = queries[..., half_dim:]
    return jnp.concatenate(
        [
            lower_part * cosine - upper_part * sine_table,
            upper_part * cosine + lower_part * sine_table,
        ],
        axis=-1,
    )


def rank_total(partial_value):
    return taken_together(partial_value, "tensor")


def body(
    hidden,
    norm_gain,
    query_matrix,
    output_weight,
    kv_pages,
    page_order,
    page_counts,
    page_trims,
    adapter_store,
    store_route,
    store_slot,
):
    tensor_size = lax.axis_size("tensor")
    group_size = lax.axis_size("group")
    shard_tensor_index = lax.axis_index("tensor")
    group_index = lax.axis_index("group")
    row_count = hidden.shape[0]
    local_width = query_matrix.shape[1]
    heads_dev = local_width // HD
    split_count = tensor_size // KVH
    part_index = shard_tensor_index % split_count
    pool_size = kv_pages.shape[0]
    half_size = kv_pages.shape[2]
    stored = adapter_store.shape[0]
    lane_count = adapter_store.shape[2]
    adapter_rank_width = lane_count // 4
    seg_count = row_count // SEG
    capacity = max(2, (2 * seg_count + group_size - 1) // group_size)
    hidden_float32 = hidden.astype(jnp.float32)
    inv_rms = lax.rsqrt(jnp.mean(hidden_float32 * hidden_float32, axis=1, keepdims=True) + norm_eps)
    normalized_hidden = (hidden_float32 * inv_rms * norm_gain.astype(jnp.float32)[None, :]).astype(
        jnp.bfloat16
    )
    normalized_local = lax.dynamic_slice_in_dim(
        normalized_hidden, shard_tensor_index * local_width, local_width, 1
    )
    route_table = store_route[:, 0].reshape(group_size, seg_count)
    slot_table = store_slot.reshape(group_size, seg_count)
    earlier = jnp.arange(seg_count)[:, None] > jnp.arange(seg_count)[None, :]
    same_route = route_table[:, :, None] == route_table[:, None, :]
    slot_rank = jnp.sum(jnp.where(same_route & earlier[None, :, :], 1, 0), axis=2).astype(jnp.int32)
    target = route_table * capacity + slot_rank
    own_target = lax.dynamic_index_in_dim(target, group_index, 0, keepdims=False)
    placing = (jnp.arange(group_size * capacity)[:, None] == own_target[None, :]).astype(
        jnp.bfloat16
    )
    wanted = (route_table == group_index)[:, :, None] & (
        slot_rank[:, :, None] == jnp.arange(capacity)[None, None, :]
    )
    slot_hot = slot_table[:, :, None] == jnp.arange(stored)[None, None, :]
    choosing = (
        jnp.einsum("gkc,gka->gca", wanted.astype(jnp.float32), slot_hot.astype(jnp.float32))
        .reshape(group_size * capacity, stored)
        .astype(jnp.bfloat16)
    )
    store_flat = adapter_store.reshape(stored, local_width * lane_count)
    outgoing = jnp.dot(choosing, store_flat, preferred_element_type=jnp.float32).astype(
        jnp.bfloat16
    )
    arrived = lax.all_to_all(
        outgoing.reshape(group_size, capacity * local_width, lane_count),
        "group",
        split_axis=0,
        concat_axis=0,
        tiled=True,
    )
    own_pages = (
        jnp.dot(
            placing.T,
            arrived.reshape(group_size * capacity, local_width * lane_count),
            preferred_element_type=jnp.float32,
        )
        .astype(jnp.bfloat16)
        .reshape(seg_count, local_width, lane_count)
    )

    def apply_adapter_update(input_rows, leading_column, trailing_column):
        segment_rows = input_rows.reshape(seg_count, SEG, local_width)
        partial_value = jnp.einsum(
            "ksd,kdr->ksr",
            segment_rows,
            own_pages[:, :, leading_column : leading_column + adapter_rank_width],
            preferred_element_type=jnp.float32,
        )
        low_rank = rank_total(partial_value).astype(jnp.bfloat16)
        result = jnp.einsum(
            "ksr,kdr->ksd",
            low_rank,
            own_pages[:, :, trailing_column : trailing_column + adapter_rank_width],
            preferred_element_type=jnp.float32,
        )
        return result.reshape(row_count, local_width)

    lengths = page_counts[0] * split_count * half_size - page_trims[0]
    query_float32 = jnp.dot(
        normalized_hidden, query_matrix, preferred_element_type=jnp.float32
    ) + adapter_scale * apply_adapter_update(normalized_local, 0, 2 * adapter_rank_width)
    queries = rotate(
        query_float32.reshape(row_count, heads_dev, HD), (lengths - 1).astype(jnp.float32)
    ).astype(jnp.bfloat16)
    level_bit = 0
    partner = partner_2(queries, "tensor", level_bit)
    upper_bit = shard_tensor_index // 2**level_bit % 2
    queries = jnp.where(
        upper_bit == 0,
        jnp.concatenate([queries, partner], axis=1),
        jnp.concatenate([partner, queries], axis=1),
    )
    offsets = jnp.cumsum(page_counts[0]) - page_counts[0]
    page_slot = jnp.clip(
        offsets[:, None] + jnp.arange(PAGES_MAX, dtype=jnp.int32)[None, :], 0, pool_size - 1
    )
    page_ids = page_order[0][page_slot]
    cached = kv_pages[:, 0][page_ids].reshape(row_count, PAGES_MAX * half_size, 2 * HD)
    positions = (
        jnp.arange(PAGES_MAX, dtype=jnp.int32)[:, None] * (split_count * half_size)
        + part_index * half_size
        + jnp.arange(half_size, dtype=jnp.int32)[None, :]
    ).reshape(-1)
    usable = positions[None, :] < lengths[:, None]
    scores = jnp.einsum(
        "rgd,rpd->rgp", queries, cached[..., :HD], preferred_element_type=jnp.float32
    ) / math.sqrt(HD)
    masked = jnp.where(usable[:, None, :], scores, -1e30)
    row_max = jnp.max(masked, axis=2)
    weights = jnp.where(usable[:, None, :], jnp.exp(masked - row_max[..., None]), 0.0).astype(
        jnp.bfloat16
    )
    totals = jnp.sum(weights.astype(jnp.float32), axis=2)
    output_part = jnp.einsum(
        "rgp,rpd->rgd", weights, cached[..., HD:], preferred_element_type=jnp.float32
    )
    level_bit = 0
    other_out = partner_2(output_part.astype(jnp.bfloat16), "tensor", level_bit).astype(
        output_part.dtype
    )
    other_max = partner_2(row_max.astype(jnp.bfloat16), "tensor", level_bit).astype(row_max.dtype)
    other_total = partner_2(totals.astype(jnp.bfloat16), "tensor", level_bit).astype(totals.dtype)
    joint_max = jnp.maximum(row_max, other_max)
    own_scale = jnp.exp(row_max - joint_max)
    other_scale = jnp.exp(other_max - joint_max)
    output_part = output_part * own_scale[..., None] + other_out * other_scale[..., None]
    totals = totals * own_scale + other_total * other_scale
    attended_all = output_part / totals[..., None]
    attention_result = (
        lax.dynamic_slice_in_dim(attended_all, part_index * heads_dev, heads_dev, 1)
        .reshape(row_count, local_width)
        .astype(jnp.bfloat16)
    )
    partial_output = jnp.dot(attention_result, output_weight, preferred_element_type=jnp.float32)
    adapter_output = adapter_scale * apply_adapter_update(
        attention_result, adapter_rank_width, 3 * adapter_rank_width
    )
    own_cols = (
        lax.dynamic_slice_in_dim(partial_output, shard_tensor_index * local_width, local_width, 1)
        + adapter_output
    )
    partial_output = lax.dynamic_update_slice_in_dim(
        partial_output, own_cols, shard_tensor_index * local_width, 1
    )
    share = sum_at_owner(partial_output.astype(jnp.bfloat16), "tensor", 1)
    own_hidden = lax.dynamic_slice_in_dim(
        hidden_float32, shard_tensor_index * local_width, local_width, 1
    )
    finished = (own_hidden + share).astype(jnp.bfloat16)
    layer_out = gathered_copies(finished, "tensor", 1)
    return layer_out


def solution(mesh):
    in_specs = (
        P("group", None),
        P(),
        P(None, "tensor"),
        P("tensor", None),
        P("group", "tensor", None, None),
        P("group", None),
        P("group", None),
        P("group", None),
        P("group", "tensor", None),
        P(),
        P(),
    )
    out_specs = P("group", None)
    return jax.shard_map(body, mesh=mesh, in_specs=in_specs, out_specs=out_specs, check_vma=False)
```

profile of v0, /device:TPU:0, one launch (start us, length us, event | category | flops | bytes accessed | tf_op | source)
XLA Modules:
  0.0 240.0 jit_solution(12726223557344055686)
XLA Ops:
  3.2 2.8 %copy.73 = bf16[1,8,512,256]{3,1,2,0:T(8,128)(2,1)S(1)} copy(bf16[1,8,512,256]{3,2,1,0:T(8,128)(2,1)} %bitcast.61) | data formatting | bytes 4194304
  6.2 3.2 %convolution_convert_fusion = bf16[16,131072]{1,0:T(8,128)(2,1)} fusion(bf16[16,8]{1,0:T(8,128)(2,1)S(1)} %bitcast.65, bf16[8,131072]{1,0:T(8,128)(2,1)S(1)} %bitcast.60), kind=kOutput, calls=%fused_computation.2 | convolution fusion | flops 35651584 | bytes 6291712 | tf_op jit(solution)/shard_map/dot_general | solution.py:133
  9.3 4.8 %reshape.277 = bf16[8,1024,256]{2,1,0:T(8,128)(2,1)} reshape(bf16[16,131072]{1,0:T(8,128)(2,1)} %convolution_convert_fusion) | data formatting | bytes 8388608 | tf_op jit(solution)/shard_map/reshape | solution.py:137
  14.2 4.7 %all-to-all-start = ((bf16[8,1024,256]{2,1,0:T(8,128)(2,1)}), bf16[8,1024,256]{2,1,0:T(8,128)(2,1)}, u32[]{:S(2)}, u32[]{:S(2)}) async-start(bf16[8,1024,256]{2,1,0:T(8,128)(2,1)} %reshape.277), calls=%async_computation | async-start | bytes 8388608 | tf_op jit(solution)/shard_map/all_to_all | solution.py:136
  19.7 6.8 %gather_fusion = s32[1024]{0:T(1024)S(1)} fusion(s32[192]{0:T(256)S(1)} %bitcast.53, s32[1024]{0:T(1024)S(1)} %broadcast_clamp_fusion), kind=kCustom, calls=%fused_computation | custom fusion | bytes 12288 | tf_op jit(solution)/shard_map/gather | solution.py:189
  26.8 2.1 multiply_reduce_fusion
  28.9 2.2 multiply_convert_fusion
  32.4 36.1 %all-to-all-done = bf16[8,1024,256]{2,1,0:T(8,128)(2,1)} async-done(((bf16[8,1024,256]{2,1,0:T(8,128)(2,1)}), bf16[8,1024,256]{2,1,0:T(8,128)(2,1)}, u32[]{:S(2)}, u32[]{:S(2)}) %all-to-all-start) | async-done | bytes 4194336 | tf_op jit(solution)/shard_map/all_to_all | solution.py:136
  68.5 4.8 %reshape.278 = bf16[16,131072]{1,0:T(8,128)(2,1)} reshape(bf16[8,1024,256]{2,1,0:T(8,128)(2,1)} %all-to-all-done) | data formatting | bytes 8388608 | tf_op jit(solution)/shard_map/reshape | solution.py:146
  73.4 2.9 %convolution_convert_fusion.1 = bf16[8,131072]{1,0:T(8,128)(2,1)S(1)} fusion(bf16[16,131072]{1,0:T(8,128)(2,1)} %reshape.278, s32[8]{0:T(128)S(1)} %fusion.41), kind=kOutput, calls=%fused_computation.3 | convolution fusion | flops 34603136 | bytes 6291488 | tf_op jit(solution)/shard_map/dot_general | solution.py:144
  76.3 2.4 %fusion.46 = (bf16[8,512,64]{2,0,1:T(8,128)(2,1)}, bf16[8,512,64]{2,0,1:T(8,128)(2,1)}, bf16[8,512,64]{2,0,1:T(8,128)(2,1)S(1)}, bf16[8,512,64]{2,0,1:T(8,128)(2,1)}) fusion(bf16[8,512,256]{2,0,1:T(8,128)(2,1)S(1)} %bitcast.56), kind=kLoop, calls=%fused_computation.92 | loop fusion | bytes 4194304 | tf_op jit(solution)/shard_map/slice | solution.py:158
  80.2 2.7 %reshape.316 = f32[16,1,8192]{2,1,0:T(1,128)} reshape(f32[16,8,16,64]{3,2,1,0:T(8,128)} %broadcast_in_dim.31) | data formatting | bytes 1048576
  82.8 8.2 %all-to-all-start.1 = ((f32[16,1,8192]{2,1,0:T(1,128)}), f32[16,1,8192]{2,1,0:T(1,128)}, u32[]{:S(2)}, u32[]{:S(2)}) async-start(f32[16,1,8192]{2,1,0:T(1,128)} %reshape.316), calls=%async_computation.1 | async-start | bytes 1048576 | tf_op jit(solution)/shard_map/all_to_all | solution.py:21
  91.1 12.4 %gather_fusion.1 = bf16[1024,32,256]{2,1,0:T(8,128)(2,1)} fusion(bf16[192,32,256]{2,1,0:T(8,128)(2,1)S(1)} %bitcast.52, s32[1024]{0:T(1024)S(1)} %broadcast_clamp_fusion.1), kind=kCustom, calls=%fused_computation.1 | custom fusion | bytes 33558528 | tf_op jit(solution)/shard_map/gather | solution.py:190
  104.4 3.7 %reduce.5 = f32[16,8192]{1,0:T(8,128)} reduce(f32[16,1,8192]{2,1,0:T(1,128)} %all-to-all-done.1, f32[]{:T(128)} %broadcast.220), dimensions={1}, to_apply=%all_to_all.16.reduce_sub_computation | reduce | bytes 1048580 | tf_op jit(solution)/shard_map/all_to_all | solution.py:21
  111.3 4.6 %convolution_add_fusion = f32[128,512]{1,0:T(8,128)S(1)} fusion(f32[128,512]{1,0:T(8,128)S(1)} %bitcast.63, bf16[128,8192]{1,0:T(8,128)(2,1)S(1)} %copy-done.5, bf16[8192,512]{1,0:T(8,128)(2,1)} %param.13), kind=kOutput, calls=%fused_computation.16 | convolution fusion | flops 1073807360 | bytes 11010048 | tf_op jit(solution)/shard_map/dot_general | solution.py:171
  116.6 1.9 collective-permute-start
  118.6 3.0 %collective-permute-done = bf16[128,4,128]{2,1,0:T(4,128)(2,1)S(1)} collective-permute-done((bf16[128,4,128]{2,1,0:T(4,128)(2,1)S(1)}, bf16[128,4,128]{2,1,0:T(4,128)(2,1)S(1)}, u32[]{:S(2)}, u32[]{:S(2)}) %collective-permute-start) | collective-permute-done | bytes 131104 | tf_op jit(solution)/shard_map/ppermute | solution.py:30
  121.6 5.8 %fusion.47 = (f32[128,8]{1,0:T(8,128)S(1)}, f32[128,8,256]{2,1,0:T(8,128)S(1)}) fusion(bf16[128,256,256]{2,1,0:T(8,128)(2,1)} %bitcast.54, bf16[128,4,128]{2,1,0:T(4,128)(2,1)S(1)} %collective-permute-done, bf16[128,4,64]{2,1,0:T(4,128)(2,1)S(1)} %get-tuple-element.15, bf16[128,4,64]{2,1,0:T(4,128)(2,1)S(1)} %get-tuple-element.14, pred[]{:T(512)S(6)} %eq.72, ...), kind=kOutput, calls=%fused_computation.93 | convolution fusion | flops 69598208 | bytes 9736193 | tf_op jit(solution)/shard_map/rgd,rpd->rgp/dot_general | solution.py:197
  128.0 1.9 collective-permute-start.3
  130.1 4.7 %fusion.48 = (bf16[128,8,128]{2,1,0:T(8,128)(2,1)S(1)}, f32[128,8,128]{2,1,0:T(8,128)S(1)}) fusion(bf16[128,256,256]{2,1,0:T(8,128)(2,1)} %bitcast.55, f32[128,8,256]{2,1,0:T(8,128)S(1)} %get-tuple-element.20, f32[128,8]{1,0:T(8,128)S(1)} %get-tuple-element.19, pred[128,256]{1,0:T(8,128)(4,1)S(1)} %broadcast_compare_fusion), kind=kOutput, calls=%fused_computation.94 | convolution fusion | flops 68026368 | bytes 10260480 | tf_op jit(solution)/shard_map/rgp,rpd->rgd/dot_general | solution.py:206
  137.1 4.1 %collective-permute-done.2 = bf16[128,8,128]{2,1,0:T(8,128)(2,1)S(1)} collective-permute-done((bf16[128,8,128]{2,1,0:T(8,128)(2,1)S(1)}, bf16[128,8,128]{2,1,0:T(8,128)(2,1)S(1)}, u32[]{:S(2)}, u32[]{:S(2)}) %collective-permute-start.2) | collective-permute-done | bytes 262176 | tf_op jit(solution)/shard_map/ppermute | solution.py:30
  143.6 7.1 %all-to-all-start.2 = ((f32[16,1,8192]{2,1,0:T(1,128)}), f32[16,1,8192]{2,1,0:T(1,128)S(1)}, u32[]{:S(2)}, u32[]{:S(2)}) async-start(f32[16,1,8192]{2,1,0:T(1,128)} %reshape.318), calls=%async_computation.2 | async-start | bytes 1048576 | tf_op jit(solution)/shard_map/all_to_all | solution.py:21
  150.7 6.7 %fusion.29 = f32[128,8192]{1,0:T(8,128)} fusion(bf16[512,8192]{1,0:T(8,128)(2,1)} %param.14, bf16[16,8,4,128]{3,2,1,0:T(4,128)(2,1)S(1)} %bitcast.62), kind=kOutput, calls=%fused_computation.47 | convolution fusion | flops 1073741824 | bytes 12713984 | tf_op jit(solution)/shard_map/dot_general | solution.py:226
  157.4 3.4 %all-to-all-done.2 = f32[16,1,8192]{2,1,0:T(1,128)S(1)} async-done(((f32[16,1,8192]{2,1,0:T(1,128)}), f32[16,1,8192]{2,1,0:T(1,128)S(1)}, u32[]{:S(2)}, u32[]{:S(2)}) %all-to-all-start.2) | async-done | bytes 524320 | tf_op jit(solution)/shard_map/all_to_all | solution.py:21
  165.3 2.4 %convert_element_type.110 = bf16[128,8192]{1,0:T(8,128)(2,1)S(1)} convert(f32[128,8192]{1,0:T(8,128)} %constant_dynamic-update-slice_fusion) | non-fusion elementwise | flops 1048576 | bytes 6291456 | tf_op jit(solution)/shard_map/convert_element_type | solution.py:237
  169.3 4.4 %all-to-all-start.3 = ((bf16[16,128,512]{2,1,0:T(8,128)(2,1)}), bf16[16,128,512]{2,1,0:T(8,128)(2,1)}, u32[]{:S(2)}, u32[]{:S(2)}) async-start(bf16[16,128,512]{2,1,0:T(8,128)(2,1)} %bitcast.58), calls=%async_computation.3 | async-start | bytes 4194304 | tf_op jit(solution)/shard_map/all_to_all | solution.py:41
  173.7 2.4 convert_element_type.88
  176.1 21.7 %all-to-all-done.3 = bf16[16,128,512]{2,1,0:T(8,128)(2,1)} async-done(((bf16[16,128,512]{2,1,0:T(8,128)(2,1)}), bf16[16,128,512]{2,1,0:T(8,128)(2,1)}, u32[]{:S(2)}, u32[]{:S(2)}) %all-to-all-start.3) | async-done | bytes 2097184 | tf_op jit(solution)/shard_map/all_to_all | solution.py:41
  200.9 31.1 %all_to_all.25 = bf16[16,128,512]{2,1,0:T(8,128)(2,1)} all-to-all(bf16[16,128,512]{2,1,0:T(8,128)(2,1)S(1)} %broadcast_in_dim.39), channel_id=1, replica_groups=mesh['group'=8,'tensor'=16] {'tensor'}, dimensions={0} | all-to-all | bytes 4194304 | tf_op jit(solution)/shard_map/all_to_all | solution.py:21
  232.1 3.9 %copy.66 = bf16[16,128,512]{1,2,0:T(8,128)(2,1)} copy(bf16[16,128,512]{2,1,0:T(8,128)(2,1)} %all_to_all.25) | data formatting | bytes 4194304 | tf_op jit(solution)/shard_map/all_to_all | solution.py:21
  236.0 4.1 %copy.67 = bf16[128,8192]{1,0:T(8,128)(2,1)} copy(bf16[128,8192]{0,1:T(8,128)(2,1)} %bitcast.59) | data formatting | bytes 4194304 | tf_op jit(solution)/shard_map/reshape | solution.py:48
  (91 shorter events, 26.3 us)
Async XLA Ops:
  0.0 91.1 %copy-start = (bf16[192,1,32,256]{3,2,1,0:T(8,128)(2,1)S(1)}, bf16[192,1,32,256]{3,2,1,0:T(8,128)(2,1)}, u32[]{:S(2)}) copy-start(bf16[192,1,32,256]{3,2,1,0:T(8,128)(2,1)} %param.15) | copy-start | bytes 9437188
  14.2 4.7 %copy-start.8 = (bf16[8192]{0:T(1024)(128)(2,1)S(1)}, bf16[8192]{0:T(1024)(128)(2,1)}, u32[]{:S(2)}) copy-start(bf16[8192]{0:T(1024)(128)(2,1)} %param.12) | copy-start | bytes 49156
  14.2 4.8 %copy-start.9 = (s32[1,128]{1,0:T(1,128)S(1)}, s32[1,128]{1,0:T(1,128)}, u32[]{:S(2)}) copy-start(s32[1,128]{1,0:T(1,128)} %param.17) | copy-start | bytes 1540
  14.2 5.3 %copy-start.10 = (s32[1,128]{1,0:T(1,128)S(1)}, s32[1,128]{1,0:T(1,128)}, u32[]{:S(2)}) copy-start(s32[1,128]{1,0:T(1,128)} %param.18) | copy-start | bytes 1540
  14.2 5.5 %copy-start.2 = (s32[1,192]{1,0:T(1,128)S(1)}, s32[1,192]{1,0:T(1,128)}, u32[]{:S(2)}) copy-start(s32[1,192]{1,0:T(1,128)} %param.16) | copy-start | bytes 2308
  14.2 54.3 %all-to-all-start = ((bf16[8,1024,256]{2,1,0:T(8,128)(2,1)}), bf16[8,1024,256]{2,1,0:T(8,128)(2,1)}, u32[]{:S(2)}, u32[]{:S(2)}) async-start(bf16[8,1024,256]{2,1,0:T(8,128)(2,1)} %reshape.277), calls=%async_computation | async-start | bytes 8388608 | tf_op jit(solution)/shard_map/all_to_all | solution.py:136
  31.1 1.3 copy-start.4
  82.8 21.0 %all-to-all-start.1 = ((f32[16,1,8192]{2,1,0:T(1,128)}), f32[16,1,8192]{2,1,0:T(1,128)}, u32[]{:S(2)}, u32[]{:S(2)}) async-start(f32[16,1,8192]{2,1,0:T(1,128)} %reshape.316), calls=%async_computation.1 | async-start | bytes 1048576 | tf_op jit(solution)/shard_map/all_to_all | solution.py:21
  103.6 7.8 %copy-start.5 = (bf16[128,8192]{1,0:T(8,128)(2,1)S(1)}, bf16[128,8192]{1,0:T(8,128)(2,1)}, u32[]{:S(2)}) copy-start(bf16[128,8192]{1,0:T(8,128)(2,1)} %copy-done.4) | copy-start | bytes 6291460
  116.6 5.0 %collective-permute-start = (bf16[128,4,128]{2,1,0:T(4,128)(2,1)S(1)}, bf16[128,4,128]{2,1,0:T(4,128)(2,1)S(1)}, u32[]{:S(2)}, u32[]{:S(2)}) collective-permute-start(bf16[128,4,128]{2,1,0:T(4,128)(2,1)S(1)} %pad_maximum_fusion), channel_id=1, source_target_pairs={{0,1},{1,0},{2,3},{3,2},{4,5},{5,4},{6,7},{7,6},{8,9},{9,8},{10,11... | collective-permute-start | bytes 393224 | tf_op jit(solution)/shard_map/ppermute | solution.py:30
  128.0 8.7 %collective-permute-start.3 = (bf16[128,8]{0,1:T(8,128)(2,1)S(1)}, bf16[128,8]{0,1:T(8,128)(2,1)S(1)}, u32[]{:S(2)}, u32[]{:S(2)}) collective-permute-start(bf16[128,8]{0,1:T(8,128)(2,1)S(1)} %convert_element_type.104), channel_id=1, source_target_pairs={{0,1},{1,0},{2,3},{3,2},{4,5},{5,4},{6,7},{7,6},{8,9},{9,8},{10,11... | collective-permute-start | bytes 6152 | tf_op jit(solution)/shard_map/ppermute | solution.py:30
  129.9 11.9 %copy-start.7 = (bf16[8,512,64]{2,0,1:T(8,128)(2,1)S(1)}, bf16[8,512,64]{2,0,1:T(8,128)(2,1)}, u32[]{:S(2)}) copy-start(bf16[8,512,64]{2,0,1:T(8,128)(2,1)} %get-tuple-element.10) | copy-start | bytes 1572868
  129.9 6.7 %collective-permute-start.1 = (bf16[128,8]{0,1:T(8,128)(2,1)S(1)}, bf16[128,8]{0,1:T(8,128)(2,1)S(1)}, u32[]{:S(2)}, u32[]{:S(2)}) collective-permute-start(bf16[128,8]{0,1:T(8,128)(2,1)S(1)} %convert_element_type.99), channel_id=1, source_target_pairs={{0,1},{1,0},{2,3},{3,2},{4,5},{5,4},{6,7},{7,6},{8,9},{9,8},{10,11... | collective-permute-start | bytes 6152 | tf_op jit(solution)/shard_map/ppermute | solution.py:30
  134.8 6.4 %collective-permute-start.2 = (bf16[128,8,128]{2,1,0:T(8,128)(2,1)S(1)}, bf16[128,8,128]{2,1,0:T(8,128)(2,1)S(1)}, u32[]{:S(2)}, u32[]{:S(2)}) collective-permute-start(bf16[128,8,128]{2,1,0:T(8,128)(2,1)S(1)} %get-tuple-element.21), channel_id=1, source_target_pairs={{0,1},{1,0},{2,3},{3,2},{4,5},{5,4},{6,7},{7,6},{8,9},{9,8},{10,11... | collective-permute-start | bytes 786440 | tf_op jit(solution)/shard_map/ppermute | solution.py:30
  143.6 17.2 %all-to-all-start.2 = ((f32[16,1,8192]{2,1,0:T(1,128)}), f32[16,1,8192]{2,1,0:T(1,128)S(1)}, u32[]{:S(2)}, u32[]{:S(2)}) async-start(f32[16,1,8192]{2,1,0:T(1,128)} %reshape.318), calls=%async_computation.2 | async-start | bytes 1048576 | tf_op jit(solution)/shard_map/all_to_all | solution.py:21
  150.7 12.5 %copy-start.6 = (bf16[8,512,64]{2,0,1:T(8,128)(2,1)S(1)}, bf16[8,512,64]{2,0,1:T(8,128)(2,1)}, u32[]{:S(2)}) copy-start(bf16[8,512,64]{2,0,1:T(8,128)(2,1)} %get-tuple-element.13) | copy-start | bytes 1572868
  167.7 6.0 %copy-start.3 = (bf16[128,8192]{1,0:T(8,128)(2,1)S(1)}, bf16[128,8192]{1,0:T(8,128)(2,1)}, u32[]{:S(2)}) copy-start(bf16[128,8192]{1,0:T(8,128)(2,1)} %param.11) | copy-start | bytes 6291460
  169.3 28.5 %all-to-all-start.3 = ((bf16[16,128,512]{2,1,0:T(8,128)(2,1)}), bf16[16,128,512]{2,1,0:T(8,128)(2,1)}, u32[]{:S(2)}, u32[]{:S(2)}) async-start(bf16[16,128,512]{2,1,0:T(8,128)(2,1)} %bitcast.58), calls=%async_computation.3 | async-start | bytes 4194304 | tf_op jit(solution)/shard_map/all_to_all | solution.py:41
  200.9 39.1 %copy-start.1 = (bf16[192,1,32,256]{3,2,1,0:T(8,128)(2,1)S(1)}, bf16[192,1,32,256]{3,2,1,0:T(8,128)(2,1)}, u32[]{:S(2)}) copy-start(bf16[192,1,32,256]{3,2,1,0:T(8,128)(2,1)} %param.15) | copy-start | bytes 9437188
where the time goes:
time: 241 us; the launch traced here: 240 us
  waiting for transfers between devices  68.4 us (28%)
  local copies, waits for them, and re-layouts  55.6 us (23%)
  blocking collectives  31.1 us (13%)
  matrix products  30.7 us (13%)
  starting transfers between devices  30.3 us (13%)
  other arithmetic  23.6 us (10%)
    all_to_all x1, waiting for transfers between devices, body(): lax.all_to_all(outgoing.reshape(group_size, capacity * local_width, lane_...  36.1 us
    all_to_all x1, blocking collectives, copy_for_each(): return lax.all_to_all(copies, axis, split_axis=0, concat_axis=0, tiled=True)  31.1 us
    all_to_all x1, waiting for transfers between devices, sum_at_owner(): lax.all_to_all(pieces, axis, split_axis=0, concat_axis=0, tiled=True)  21.7 us
    all_to_all x2, starting transfers between devices, copy_for_each(): return lax.all_to_all(copies, axis, split_axis=0, concat_axis=0, tiled=True)  15.3 us
    gather x1, local copies, waits for them, and re-layouts, body(): kv_pages[:, 0][page_ids].reshape(row_count, PAGES_MAX * half_size, 2 * HD)  12.4 us
    unnamed x28, local copies, waits for them, and re-layouts  10.6 us
    ppermute x4, waiting for transfers between devices, partner_2(): lax.ppermute(value, axis, [(i, i ^ 1 << stride) for i in range(lax.axis_s...  7.09 us
    gather x2, local copies, waits for them, and re-layouts, body(): page_ids = page_order[0][page_slot]  6.91 us
  transfers between devices with their start and end apart: 8, of which 5 were waited for; matrix products, arithmetic and copies ran while one was open for 16% of the time, Pallas kernels for 0%

commit v1 on v0

v1 whole, which is shorter than its diff:
```python
import functools
import math

import jax
import jax.numpy as jnp
from jax import lax
from jax.experimental import pallas as pl
from jax.experimental.pallas import tpu as pltpu
from jax.sharding import PartitionSpec as P

MESH = pl.DeviceIdType.MESH
F32 = jnp.float32
BF16 = jnp.bfloat16

KVH = 8
HD = 128
SEG = 16
SIDE = 4
NB = 256
adapter_scale = 2.0
norm_eps = 1e-05
rope_base = 500000.0
far_score = -1e30
orders = (2, 1, 3, 0)


def iota(shape, dim):
    return lax.broadcasted_iota(jnp.int32, shape, dim)


def dot(a, b):
    return jnp.dot(a, b, preferred_element_type=F32)


def dot_nt(a, b):
    return lax.dot_general(a, b, (((1,), (1,)), ((), ())), preferred_element_type=F32)


def enter(sizes, g, t):
    groups, tensors = sizes
    barrier = pltpu.get_barrier_semaphore()

    def greet_tensor(d, c):
        pl.semaphore_signal(
            barrier, inc=1, device_id=(g, lax.rem(t + d, tensors)), device_id_type=MESH
        )
        return c

    def greet_group(d, c):
        pl.semaphore_signal(
            barrier, inc=1, device_id=(lax.rem(g + d, groups), t), device_id_type=MESH
        )
        return c

    lax.fori_loop(1, tensors, greet_tensor, 0)
    lax.fori_loop(1, groups, greet_group, 0)
    return lambda: pl.semaphore_wait(barrier, groups + tensors - 2)


def selection(route_ref, slot_ref, g, groups, cap):
    slot_rows = groups * cap * SEG
    segs = groups * 8
    rc = route_ref[pl.ds(pl.multiple_of(g * 8, 8), 8), :].astype(F32)
    lane, sub = iota((8, 128), 1), iota((8, 128), 0)
    own_seg = lane >> 4
    r_row = jnp.sum(jnp.where(own_seg == sub, rc, 0.0), axis=0, keepdims=True)
    rank = jnp.sum(
        jnp.where((rc == r_row) & (sub < own_seg), 1.0, 0.0), axis=0, keepdims=True
    )
    in_seg = (iota((1, 128), 1) & 15).astype(F32)
    spot = (r_row * cap + rank) * SEG + in_seg
    place = jnp.where(iota((slot_rows, 128), 0).astype(F32) == spot, 1.0, 0.0)
    lane, sub = iota((segs, 128), 1), iota((segs, 128), 0)
    mine = jnp.where(route_ref[...] == g, 1.0, 0.0)
    slots = slot_ref[...].astype(F32)
    diag = lane == sub
    mine_row = jnp.sum(jnp.where(diag, mine, 0.0), axis=0, keepdims=True)
    rank = jnp.sum(
        jnp.where(((lane >> 3) == (sub >> 3)) & (lane < sub), mine_row, 0.0),
        axis=1,
        keepdims=True,
    )
    spot = mine * ((iota((segs, 1), 0) >> 3).astype(F32) * cap + rank + 1.0)
    spot_row = jnp.sum(jnp.where(diag, spot, 0.0), axis=0, keepdims=True)
    value_row = jnp.sum(jnp.where(diag, slots + 1.0, 0.0), axis=0, keepdims=True)
    row_slot = (iota((slot_rows, 128), 0) >> 4).astype(F32) + 1.0
    adapter = jnp.sum(jnp.where(spot_row == row_slot, value_row, 0.0), axis=1, keepdims=True) - 1.0
    return place, adapter


class Lora:
    def __init__(self, refs, sizes, g, t, cap):
        (
            self.xs, self.xr, self.ps, self.pr, self.ks, self.ka, self.ds, self.dr,
            self.ssem, self.rsem,
        ) = refs
        self.groups, self.tensors = sizes
        self.g, self.t, self.cap = g, t, cap
        self.rows = cap * SEG

    def pair_copy(self, src, dst, stage, peer, at):
        return pltpu.make_async_remote_copy(
            src_ref=src, dst_ref=dst,
            send_sem=self.ssem.at[stage, peer], recv_sem=self.rsem.at[stage, at],
            device_id=(peer, self.t) if stage % 2 == 0 else (self.g, peer),
            device_id_type=MESH,
        )

    def start(self, src_of, dst, stage):
        me, n = (self.g, self.groups) if stage % 2 == 0 else (self.t, self.tensors)

        def send(d, c):
            peer = lax.rem(me + d, n)
            self.pair_copy(src_of(peer), dst.at[me], stage, peer, me).start()
            return c

        lax.fori_loop(1, n, send, 0)

    def finish(self, src_of, dst, stage):
        me, n = (self.g, self.groups) if stage % 2 == 0 else (self.t, self.tensors)

        def end(d, c):
            peer = lax.rem(me + d, n)
            self.pair_copy(src_of(peer), dst.at[peer], stage, peer, peer).wait()
            return c

        lax.fori_loop(1, n, end, 0)

    def send_rows(self, place, local):
        picked = dot(place.astype(BF16), local).astype(BF16)
        for s in range(self.groups):
            self.xs[s] = picked[s * self.rows : (s + 1) * self.rows]
        self.start(lambda p: self.xs.at[p], self.xr, 0)
        self.xr[self.g] = self.xs[self.g]

    def send_partials(self, adapter, store):
        self.finish(lambda p: self.xs.at[p], self.xr, 0)
        rows = self.xr[...].reshape(self.groups * self.rows, self.xr.shape[2])
        total = jnp.zeros((self.groups * self.rows, 128), F32)
        for pair in range(4):
            factors = jnp.concatenate(
                [store[2 * pair, :, 0:128], store[2 * pair + 1, :, 0:128]], axis=1
            )
            both = dot(rows, factors)
            total = total + jnp.where(adapter == 2.0 * pair, both[:, 0:128], 0.0)
            total = total + jnp.where(adapter == 2.0 * pair + 1.0, both[:, 128:256], 0.0)
        own = total.shape[0] // self.tensors
        for s in range(self.tensors):
            self.ps[s] = total[s * own : (s + 1) * own]
        self.start(lambda p: self.ps.at[p], self.pr, 1)
        self.pr[self.t] = self.ps[self.t]

    def send_ranks(self, first_lane):
        self.finish(lambda p: self.ps.at[p], self.pr, 1)
        total = self.pr[0]
        for s in range(1, self.tensors):
            total = total + self.pr[s]
        lane = iota(total.shape, 1)
        total = jnp.where((lane >= first_lane) & (lane < first_lane + 64), total, 0.0)
        self.ks[...] = total.astype(BF16)
        self.start(lambda p: self.ks, self.ka, 3)
        self.ka[self.t] = self.ks[...]

    def send_updates(self, adapter, store):
        self.finish(lambda p: self.ks, self.ka, 3)
        rank = self.ka[...].reshape(self.groups * self.rows, 128).astype(F32)
        total = None
        for pair in range(4):
            low = jnp.concatenate(
                [
                    jnp.where(adapter == 2.0 * pair, rank, 0.0),
                    jnp.where(adapter == 2.0 * pair + 1.0, rank, 0.0),
                ],
                axis=1,
            ).astype(BF16)
            factors = jnp.concatenate(
                [store[2 * pair, :, 128:256], store[2 * pair + 1, :, 128:256]], axis=1
            )
            part = dot_nt(low, factors)
            total = part if total is None else total + part
        total = total.astype(BF16)
        for s in range(self.groups):
            self.ds[s] = total[s * self.rows : (s + 1) * self.rows]
        self.start(lambda p: self.ds.at[p], self.dr, 2)
        self.dr[self.g] = self.ds[self.g]

    def update(self, place):
        self.finish(lambda p: self.ds.at[p], self.dr, 2)
        rows = self.dr[...].reshape(self.groups * self.rows, self.dr.shape[2])
        return adapter_scale * dot(place.T.astype(BF16), rows)


def lora_scratch(sizes, cap, width):
    groups, tensors = sizes
    own = groups * cap * SEG // tensors
    big = max(groups, tensors)
    return [
        pltpu.VMEM((groups, cap * SEG, width), BF16),
        pltpu.VMEM((groups, cap * SEG, width), BF16),
        pltpu.VMEM((tensors, own, 128), F32),
        pltpu.VMEM((tensors, own, 128), F32),
        pltpu.VMEM((own, 128), BF16),
        pltpu.VMEM((tensors, own, 128), BF16),
        pltpu.VMEM((groups, cap * SEG, width), BF16),
        pltpu.VMEM((groups, cap * SEG, width), BF16),
        pltpu.SemaphoreType.DMA((4, big)),
        pltpu.SemaphoreType.DMA((4, big)),
    ]


def query_kernel(
    sizes, cap,
    gain_ref, cos_ref, sin_ref, route_ref, slot_ref, hidden_hbm, matrix_hbm, store_hbm,
    q_ref,
    hidden_ref, normed_ref, matrix_ref, store_ref, inv_ref, acc_ref, load_sem, pair_sem,
    *lora_refs,
):
    g, t = lax.axis_index("group"), lax.axis_index("tensor")
    chunks = matrix_ref.shape[0]
    depth = matrix_ref.shape[1]
    rows, width = hidden_ref.shape
    local_width = matrix_ref.shape[2]
    hidden_load = pltpu.make_async_copy(hidden_hbm, hidden_ref, load_sem.at[chunks])
    hidden_load.start()
    loads = [
        pltpu.make_async_copy(
            matrix_hbm.at[pl.ds(k * depth, depth), :], matrix_ref.at[k], load_sem.at[k]
        )
        for k in range(chunks)
    ]
    store_load = pltpu.make_async_copy(store_hbm, store_ref, load_sem.at[chunks + 1])
    for k in range(2):
        loads[k].start()
    store_load.start()
    for k in range(2, chunks):
        loads[k].start()
    all_in = enter(sizes, g, t)
    place, adapter = selection(route_ref, slot_ref, g, sizes[0], cap)
    lora = Lora(lora_refs, sizes, g, t, cap)
    hidden_load.wait()

    def squares(r, c):
        at = pl.ds(pl.multiple_of(r * 16, 16), 16)
        total = jnp.zeros((16, 128), F32)
        for k in range(width // 1024):
            x = hidden_ref[at, k * 1024 : (k + 1) * 1024].astype(F32)
            x = x * x
            for j in range(8):
                total = total + x[:, j * 128 : (j + 1) * 128]
        mean = jnp.sum(total, axis=1, keepdims=True) / width
        inv_ref[at, :] = jnp.broadcast_to(lax.rsqrt(mean + norm_eps), (16, 128))
        return c

    lax.fori_loop(0, rows // 16, squares, 0)
    own_cols = pl.ds(pl.multiple_of(t * local_width, local_width), local_width)
    local = (
        hidden_ref[:, own_cols].astype(F32) * inv_ref[:, 0:1] * gain_ref[:, own_cols].astype(F32)
    ).astype(BF16)
    all_in()
    lora.send_rows(place, local)

    def normalize(r, c):
        at = pl.ds(pl.multiple_of(r * 16, 16), 16)
        inv = inv_ref[at, 0:1]
        for k in range(width // 1024):
            cols = slice(k * 1024, (k + 1) * 1024)
            normed_ref[at, cols] = (
                hidden_ref[at, cols].astype(F32) * inv * gain_ref[:, cols].astype(F32)
            ).astype(BF16)
        return c

    lax.fori_loop(0, rows // 16, normalize, 0)

    def project(k):
        loads[k].wait()
        part = dot(normed_ref[:, k * depth : (k + 1) * depth], matrix_ref[k])
        acc_ref[...] = part if k == 0 else acc_ref[...] + part

    for k in range(4):
        project(k)
    store_load.wait()
    lora.send_partials(adapter, store_ref)
    for k in range(4, chunks):
        project(k)
    lora.send_ranks(0)
    lora.send_updates(adapter, store_ref)
    full = acc_ref[...] + lora.update(place)
    part = lax.rem(t, 2)
    heads = []
    for h in range(local_width // HD):
        x = full[:, h * HD : (h + 1) * HD]
        heads.append(x * cos_ref[...] + pltpu.roll(x, HD // 2, 1) * sin_ref[...])
    own_half = pl.ds(pl.multiple_of(part * local_width, local_width), local_width)
    q_ref[:, own_half] = jnp.concatenate(heads, axis=1).astype(BF16)
    other_half = pl.ds(pl.multiple_of((1 - part) * local_width, local_width), local_width)
    partner = t + 1 - 2 * part
    send = pltpu.make_async_remote_copy(
        src_ref=q_ref.at[:, own_half], dst_ref=q_ref.at[:, own_half],
        send_sem=pair_sem.at[0], recv_sem=pair_sem.at[1],
        device_id=(g, partner), device_id_type=MESH,
    )
    send.start()
    send.wait_send()
    pltpu.make_async_remote_copy(
        src_ref=q_ref.at[:, other_half], dst_ref=q_ref.at[:, other_half],
        send_sem=pair_sem.at[0], recv_sem=pair_sem.at[1],
        device_id=(g, partner), device_id_type=MESH,
    ).wait_recv()


def attend(q, kv_ref, order_ref, counts_ref, trims_ref, part, o_ref, ml_ref, work):
    own_ref, qp_ref, op_ref, mp_ref, lp_ref = work
    rows = counts_ref.shape[1]
    pool = order_ref.shape[1]
    heads = q.shape[1] // HD
    half = kv_ref.shape[0] // pool
    block = NB // half
    counts = counts_ref[...].astype(F32)
    trims = trims_ref[...].astype(F32)
    square = (rows, rows)
    diag = iota(square, 0) == iota(square, 1)
    count_col = jnp.sum(jnp.where(diag, counts, 0.0), axis=1, keepdims=True)
    offsets = jnp.sum(
        jnp.where(iota(square, 0) < iota(square, 1), count_col, 0.0), axis=0, keepdims=True
    )
    lengths = counts * (2 * half) - trims
    spot = jnp.sum(
        jnp.where(order_ref[...] == iota((pool, pool), 0), iota((pool, pool), 1).astype(F32), 0.0),
        axis=1,
        keepdims=True,
    )
    owner = (spot >= offsets) & (spot < offsets + counts)
    own_ref[...] = jnp.where(owner, 1.0, 0.0)
    first = (part * half).astype(F32)
    used = jnp.sum(
        jnp.where(owner, lengths - (spot - offsets) * (2 * half) - first, 0.0),
        axis=1,
        keepdims=True,
    )
    qp_ref[...] = dot(own_ref[...].astype(BF16), q)
    wide = (block * heads, NB)
    same_page = (iota(wide, 1) // half) == (iota(wide, 0) & (block - 1))
    slot = (iota(wide, 1) & (half - 1)).astype(F32)
    for b in range(pool // block):
        pages = slice(b * block, (b + 1) * block)
        query = jnp.concatenate(
            [qp_ref[pages, h * HD : (h + 1) * HD] for h in range(heads)], axis=0
        ).astype(BF16)
        keys = kv_ref[b * NB : (b + 1) * NB, 0:HD]
        values = kv_ref[b * NB : (b + 1) * NB, HD : 2 * HD]
        scores = dot_nt(query, keys) / math.sqrt(HD)
        limit = jnp.concatenate([used[pages]] * heads, axis=0)
        usable = same_page & (slot < limit)
        masked = jnp.where(usable, scores, far_score)
        top = jnp.max(masked, axis=1, keepdims=True)
        weights = jnp.where(usable, jnp.exp(masked - top), 0.0).astype(BF16)
        total = jnp.sum(weights.astype(F32), axis=1, keepdims=True)
        op_ref[b] = dot(weights, values)
        mp_ref[b] = jnp.broadcast_to(top, (block * heads, HD))
        lp_ref[b] = jnp.broadcast_to(total, (block * heads, HD))
    own_t = own_ref[...].T.astype(BF16)
    lane = iota((rows, HD), 1)
    summary = jnp.zeros((rows, HD), F32)
    for h in range(heads):
        inner = slice(h * block, (h + 1) * block)
        top = jnp.full((block, rows), far_score, F32)
        for b in range(pool // block):
            mine = own_ref[b * block : (b + 1) * block, :] > 0.0
            top = jnp.maximum(top, jnp.where(mine, mp_ref[b, inner, :], far_score))
        top = jnp.max(top, axis=0, keepdims=True)
        total = jnp.zeros((block, rows), F32)
        scaled = []
        for b in range(pool // block):
            mine = own_ref[b * block : (b + 1) * block, :] > 0.0
            page_top = jnp.max(jnp.where(mine, top, far_score), axis=1, keepdims=True)
            factor = jnp.exp(mp_ref[b, inner, :] - page_top)
            scaled.append(op_ref[b, inner, :] * factor)
            total = total + jnp.where(mine, lp_ref[b, inner, :] * factor, 0.0)
        total = jnp.sum(total, axis=0, keepdims=True)
        o_ref[:, h * HD : (h + 1) * HD] = dot(own_t, jnp.concatenate(scaled, axis=0).astype(BF16))
        top_col = jnp.sum(jnp.where(diag, top, 0.0), axis=1, keepdims=True)
        total_col = jnp.sum(jnp.where(diag, total, 0.0), axis=1, keepdims=True)
        summary = jnp.where(lane == h, top_col, summary)
        summary = jnp.where(lane == heads + h, total_col, summary)
    ml_ref[...] = summary


class Torus:
    def __init__(self, g, t):
        self.g, self.y, self.z = g, t // SIDE, lax.rem(t, SIDE)

    def at(self, h, da, db):
        dy, dz = (da, db) if h == 0 else (db, da)
        return lax.rem(self.y + dy, SIDE) * SIDE + lax.rem(self.z + dz, SIDE)

    def near(self, h, level, sign):
        step = 1 if sign > 0 else SIDE - 1
        return (self.g, self.at(h, step, 0) if level < 4 else self.at(h, 0, step))


def output_kernel(
    sizes, cap,
    q_ref, order_ref, counts_ref, trims_ref, route_ref, slot_ref,
    kv_hbm, weight_hbm, hidden_hbm, store_hbm,
    out_ref,
    kv_ref, weight_ref, hidden_ref, store_ref, o_ref, ml_ref,
    own_ref, qp_ref, op_ref, mp_ref, lp_ref,
    os_ref, or_ref, mr_ref, att_ref, snd, rcv, keep, mine, fin,
    load_sem, pair_sem, rs_s, rs_r, ag_s, ag_r,
    *lora_refs,
):
    g, t = lax.axis_index("group"), lax.axis_index("tensor")
    part = lax.rem(t, 2)
    partner = t + 1 - 2 * part
    width = att_ref.shape[1]
    own_cols = pl.ds(pl.multiple_of(t * width, width), width)
    loads = [
        pltpu.make_async_copy(kv_hbm, kv_ref, load_sem.at[0]),
        pltpu.make_async_copy(weight_hbm, weight_ref, load_sem.at[1]),
        pltpu.make_async_copy(store_hbm, store_ref, load_sem.at[2]),
        pltpu.make_async_copy(hidden_hbm.at[:, own_cols], hidden_ref, load_sem.at[3]),
    ]
    for load in loads:
        load.start()
    all_in = enter(sizes, g, t)
    place, adapter = selection(route_ref, slot_ref, g, sizes[0], cap)
    lora = Lora(lora_refs, sizes, g, t, cap)
    torus = Torus(g, t)
    loads[0].wait()
    attend(
        q_ref[...], kv_ref, order_ref, counts_ref, trims_ref, part, o_ref, ml_ref,
        (own_ref, qp_ref, op_ref, mp_ref, lp_ref),
    )
    all_in()

    own_half = pl.ds(pl.multiple_of(part * width, width), width)
    other_half = pl.ds(pl.multiple_of((1 - part) * width, width), width)
    os_ref[...] = o_ref[:, other_half].astype(BF16)
    pair = [
        pltpu.make_async_remote_copy(
            src_ref=src, dst_ref=dst, send_sem=pair_sem.at[0, i], recv_sem=pair_sem.at[1, i],
            device_id=(g, partner), device_id_type=MESH,
        )
        for i, (src, dst) in enumerate(((ml_ref, mr_ref), (os_ref, or_ref)))
    ]
    for copy in pair:
        copy.start()
    for copy in pair:
        copy.wait()
    lane = iota(ml_ref.shape, 1)
    for i in range(width // HD):
        cols = slice(i * HD, (i + 1) * HD)
        head = part * (width // HD) + i

        def pick(ref, first):
            return jnp.sum(jnp.where(lane == head + first, ref[...], 0.0), axis=1, keepdims=True)

        own_top, other_top = pick(ml_ref, 0), pick(mr_ref, 0)
        top = jnp.maximum(own_top, other_top)
        own_scale, other_scale = jnp.exp(own_top - top), jnp.exp(other_top - top)
        total = pick(ml_ref, 8) * own_scale + pick(mr_ref, 8) * other_scale
        own_o = o_ref[:, pl.ds(pl.multiple_of(part * width + i * HD, HD), HD)]
        joined = own_o * own_scale + or_ref[:, cols].astype(F32) * other_scale
        att_ref[:, cols] = (joined / total).astype(BF16)

    lora.send_rows(place, att_ref[...])

    def block(h, da, db):
        col = torus.at(h, da, db) * (2 * NB) + h * NB
        return dot(att_ref[...], weight_ref[:, pl.ds(pl.multiple_of(col, NB), NB)])

    def copy_of(h, level, kind):
        return pltpu.make_async_remote_copy(
            src_ref=snd.at[h, level, kind], dst_ref=rcv.at[h, level, kind],
            send_sem=rs_s.at[h, level, kind], recv_sem=rs_r.at[h, level, kind],
            device_id=torus.near(h, level, 1 if kind % 2 == 0 else -1), device_id_type=MESH,
        )

    def send(h, level, kind, value):
        snd[h, level, kind] = value.astype(BF16)
        copy_of(h, level, kind).start()

    def got(h, level, kind):
        copy_of(h, level, kind).wait_recv()
        return rcv[h, level, kind].astype(F32)

    def send_far(h, level, value):
        send(h, level, 0, value[:64])
        send(h, level, 1, value[64:])

    def send_plus(h, level, value):
        send(h, level, 2, value[64:])
        keep[h, level, 0] = value[:64]

    def send_minus(h, level, value):
        send(h, level, 3, value[:64])
        keep[h, level, 1] = value[64:]

    def relay(h, level):
        send(h, level, 4, keep[h, level, 0] + got(h, level, 0))
        send(h, level, 5, keep[h, level, 1] + got(h, level, 1))

    def arrived(h, level, value):
        upper = value[:64] + got(h, level, 3) + got(h, level, 4)
        lower = value[64:] + got(h, level, 2) + got(h, level, 5)
        return jnp.concatenate([upper, lower], axis=0)

    loads[1].wait()
    for level, db in enumerate(orders):
        for h in range(2):
            send_far(h, level, block(h, 2, db))
    for level, db in enumerate(orders):
        for h in range(2):
            send_plus(h, level, block(h, 1, db))
            send_minus(h, level, block(h, 3, db))
    loads[2].wait()
    lora.send_partials(adapter, store_ref)
    for level, db in enumerate(orders):
        for h in range(2):
            mine[h, level] = block(h, 0, db)
    for level in range(4):
        for h in range(2):
            relay(h, level)
    lora.send_ranks(64)
    for level in range(4):
        for h in range(2):
            value = arrived(h, level, mine[h, level])
            if level == 0:
                send_far(h, 4, value)
            elif level == 1:
                send_plus(h, 4, value)
            elif level == 2:
                send_minus(h, 4, value)
            else:
                fin[h] = value
    lora.send_updates(adapter, store_ref)
    for h in range(2):
        relay(h, 4)
    loads[3].wait()
    update = lora.update(place)
    for h in range(2):
        cols = slice(h * NB, (h + 1) * NB)
        total = arrived(h, 4, fin[h]) + update[:, cols] + hidden_ref[:, cols].astype(F32)
        col = t * width + h * NB
        out_ref[:, pl.ds(pl.multiple_of(col, NB), NB)] = total.astype(BF16)

    def spread(h, level, kind, da, db):
        col = torus.at(h, da, db) * (2 * NB) + h * NB
        rows = (slice(0, 128), slice(0, 128), slice(0, 64), slice(64, 128))[kind]
        place_at = out_ref.at[rows, pl.ds(pl.multiple_of(col, NB), NB)]
        return pltpu.make_async_remote_copy(
            src_ref=place_at, dst_ref=place_at,
            send_sem=ag_s.at[h, level, kind], recv_sem=ag_r.at[h, level, kind],
            device_id=torus.near(h, level, 1 if kind % 2 == 0 else -1), device_id_type=MESH,
        )

    sent = (0, 0, 3, 1)
    brought = (3, 1, 2, 2)

    def go(h, level, kind):
        if level == 4:
            spread(h, level, kind, 0, sent[kind]).start()
        else:
            spread(h, level, kind, sent[kind], level).start()

    def came(h, level, kind):
        if level == 4:
            spread(h, level, kind, 0, brought[kind]).wait_recv()
        else:
            spread(h, level, kind, brought[kind], level).wait_recv()

    def left(h, level, kind):
        if level == 4:
            spread(h, level, kind, 0, sent[kind]).wait_send()
        else:
            spread(h, level, kind, sent[kind], level).wait_send()

    def go_both(h, level):
        go(h, level, 0)
        go(h, level, 1)

    def pass_on(h, level):
        came(h, level, 0)
        go(h, level, 2)
        came(h, level, 1)
        go(h, level, 3)

    for h in range(2):
        go_both(h, 4)
    for h in range(2):
        go_both(h, 0)
    for h in range(2):
        came(h, 4, 0)
        go(h, 4, 2)
        go_both(h, 3)
        came(h, 4, 1)
        go(h, 4, 3)
        go_both(h, 1)
    for h in range(2):
        pass_on(h, 0)
    for h in range(2):
        came(h, 4, 2)
        came(h, 4, 3)
        go_both(h, 2)
    for level in (3, 1, 2):
        for h in range(2):
            pass_on(h, level)
    for level in (0, 3, 1, 2):
        for h in range(2):
            came(h, level, 2)
            came(h, level, 3)
    for level in range(5):
        for h in range(2):
            for kind in range(6):
                copy_of(h, level, kind).wait_send()
            for kind in range(4):
                left(h, level, kind)


def body(
    sizes,
    hidden, norm_gain, query_matrix, output_weight, kv_pages, page_order, page_counts,
    page_trims, adapter_store, store_route, store_slot,
):
    groups = sizes[0]
    cap = max(2, 16 // groups) if groups > 1 else 8
    rows, width = hidden.shape
    local_width = query_matrix.shape[1]
    pool, _, half, lanes = kv_pages.shape
    stored = adapter_store.shape[0]
    slots = store_slot.reshape(-1, 1)
    lengths = page_counts[0] * (2 * half) - page_trims[0]
    half_dim = HD // 2
    frequency = rope_base ** (-(jnp.arange(half_dim).astype(F32) * 2.0) / HD)
    angles = (lengths - 1).astype(F32)[:, None] * frequency[None, :]
    cosine, sine = jnp.cos(angles), jnp.sin(angles)
    cos_table = jnp.concatenate([cosine, cosine], axis=1)
    sin_table = jnp.concatenate([-sine, sine], axis=1)
    vmem = pl.BlockSpec(memory_space=pltpu.VMEM)
    anywhere = pl.BlockSpec(memory_space=pl.ANY)
    chunks = 8
    query = pl.pallas_call(
        functools.partial(query_kernel, sizes, cap),
        out_shape=jax.ShapeDtypeStruct((rows, 2 * local_width), BF16),
        in_specs=[vmem] * 5 + [anywhere] * 3,
        out_specs=vmem,
        scratch_shapes=[
            pltpu.VMEM((rows, width), BF16),
            pltpu.VMEM((rows, width), BF16),
            pltpu.VMEM((chunks, width // chunks, local_width), BF16),
            pltpu.VMEM((stored, local_width, lanes), BF16),
            pltpu.VMEM((rows, 128), F32),
            pltpu.VMEM((rows, local_width), F32),
            pltpu.SemaphoreType.DMA((chunks + 2,)),
            pltpu.SemaphoreType.DMA((2,)),
        ]
        + lora_scratch(sizes, cap, local_width),
        compiler_params=pltpu.CompilerParams(
            collective_id=0, has_side_effects=True, vmem_limit_bytes=48 << 20
        ),
        name="query_part",
    )(
        norm_gain.reshape(1, -1), cos_table, sin_table, store_route, slots,
        hidden, query_matrix, adapter_store,
    )
    blocks = pool * half // NB
    block_rows = (NB // half) * (2 * local_width // HD)
    return pl.pallas_call(
        functools.partial(output_kernel, sizes, cap),
        out_shape=jax.ShapeDtypeStruct((rows, width), BF16),
        in_specs=[vmem] * 6 + [anywhere] * 4,
        out_specs=vmem,
        scratch_shapes=[
            pltpu.VMEM((pool * half, lanes), BF16),
            pltpu.VMEM((local_width, width), BF16),
            pltpu.VMEM((rows, local_width), BF16),
            pltpu.VMEM((stored, local_width, lanes), BF16),
            pltpu.VMEM((rows, 2 * local_width), F32),
            pltpu.VMEM((rows, 128), F32),
            pltpu.VMEM((pool, rows), F32),
            pltpu.VMEM((pool, 2 * local_width), F32),
            pltpu.VMEM((blocks, block_rows, HD), F32),
            pltpu.VMEM((blocks, block_rows, HD), F32),
            pltpu.VMEM((blocks, block_rows, HD), F32),
            pltpu.VMEM((rows, local_width), BF16),
            pltpu.VMEM((rows, local_width), BF16),
            pltpu.VMEM((rows, 128), F32),
            pltpu.VMEM((rows, local_width), BF16),
            pltpu.VMEM((2, 5, 6, rows // 2, NB), BF16),
            pltpu.VMEM((2, 5, 6, rows // 2, NB), BF16),
            pltpu.VMEM((2, 5, 2, rows // 2, NB), F32),
            pltpu.VMEM((2, 4, rows, NB), F32),
            pltpu.VMEM((2, rows, NB), F32),
            pltpu.SemaphoreType.DMA((4,)),
            pltpu.SemaphoreType.DMA((2, 2)),
            pltpu.SemaphoreType.DMA((2, 5, 6)),
            pltpu.SemaphoreType.DMA((2, 5, 6)),
            pltpu.SemaphoreType.DMA((2, 5, 4)),
            pltpu.SemaphoreType.DMA((2, 5, 4)),
        ]
        + lora_scratch(sizes, cap, local_width),
        compiler_params=pltpu.CompilerParams(
            collective_id=1, has_side_effects=True, vmem_limit_bytes=48 << 20
        ),
        name="output_part",
    )(
        query, page_order, page_counts, page_trims, store_route, slots,
        kv_pages.reshape(pool * half, lanes), output_weight, hidden, adapter_store,
    )


def solution(mesh):
    sizes = (mesh.shape["group"], mesh.shape["tensor"])
    in_specs = (
        P("group", None),
        P(),
        P(None, "tensor"),
        P("tensor", None),
        P("group", "tensor", None, None),
        P("group", None),
        P("group", None),
        P("group", None),
        P("group", "tensor", None),
        P(),
        P(),
    )
    return jax.shard_map(
        functools.partial(body, sizes),
        mesh=mesh,
        in_specs=in_specs,
        out_specs=P("group", None),
        check_vma=False,
    )
```

time: 241 us -> 99.7 us (0.41)
  Pallas kernels: 0 us -> 91.5 us
  waiting for transfers between devices: 68.4 us -> 0 us
  local copies, waits for them, and re-layouts: 55.6 us -> 6.74 us
  blocking collectives: 31.1 us -> 0 us
  matrix products: 30.7 us -> 0 us
  starting transfers between devices: 30.3 us -> 0 us
  other arithmetic: 23.6 us -> 1.09 us
    pallas_call x0 -> x2, Pallas kernels: none -> 91.5 us  [the longest x1 56.8 us: body(): pl.pallas_call(functools.partial(output_kernel, sizes, cap), out_shape=ja...]
    all_to_all x4 -> x0, waiting for transfers between devices: 61.3 us -> none  [the longest x1 36.1 us: body(): lax.all_to_all(outgoing.reshape(group_size, capacity * local_width, lane_...]
    all_to_all x1 -> x0, blocking collectives: 31.1 us -> none  [copy_for_each(): return lax.all_to_all(copies, axis, split_axis=0, concat_axis=0, tiled=True)]
    dot_general x11 -> x0, matrix products: 30.7 us -> none  [the longest x1 6.66 us: body(): jnp.dot(attention_result, output_weight, preferred_element_type=jnp.float32)]
    all_to_all x4 -> x0, starting transfers between devices: 24.4 us -> none  [the longest x2 15.3 us: copy_for_each(): return lax.all_to_all(copies, axis, split_axis=0, concat_axis=0, tiled=True)]
    gather x3 -> x0, local copies, waits for them, and re-layouts: 19.4 us -> none  [the longest x1 12.4 us: body(): kv_pages[:, 0][page_ids].reshape(row_count, PAGES_MAX * half_size, 2 * HD)]
    reshape x5 -> x2, local copies, waits for them, and re-layouts: 15.4 us -> 1.48 us  [the longest x1 0.74 us: body(): slots = store_slot.reshape(-1, 1)]
    convert_element_type x9 -> x1, other arithmetic: 8.45 us -> 0.68 us  [body(): angles = (lengths - 1).astype(F32)[:, None] * frequency[None, :]]
  transfers between devices with their start and end apart: 8 -> 0, of which waited for: 5 -> 0; matrix products, arithmetic and copies ran while one was open for 16% -> 0% of each run, Pallas kernels for 0% -> 0%
where the time goes in v1:
time: 99.7 us; the launch traced here: 99.4 us
  Pallas kernels  91.5 us (92%)
  local copies, waits for them, and re-layouts  6.74 us (7%)
  other arithmetic  1.09 us (1%)
    pallas_call x1, Pallas kernels, body(): pl.pallas_call(functools.partial(output_kernel, sizes, cap), out_shape=ja...  56.8 us
    pallas_call x1, Pallas kernels, body(): pl.pallas_call(functools.partial(query_kernel, sizes, cap), out_shape=jax...  34.7 us
    unnamed x14, local copies, waits for them, and re-layouts  5.26 us

profile of v1, /device:TPU:0, one launch (start us, length us, event | category | flops | bytes accessed | tf_op | source)
XLA Modules:
  0.0 99.4 jit_solution(16828872475741620345)
XLA Ops:
  0.0 0.7 convert_bitcast_fusion
  0.7 0.7 copy.12.route_ref
  1.4 0.7 copy.13.slot_ref
  2.2 0.7 reshape.35.gain_ref
  2.9 0.3 fusion
  3.2 0.1 pad_maximum_fusion
  3.3 0.0 copy-start
  3.4 1.6 %copy-done = bf16[128,8192]{1,0:T(8,128)(2,1)S(1)} copy-done((bf16[128,8192]{1,0:T(8,128)(2,1)S(1)}, bf16[128,8192]{1,0:T(8,128)(2,1)}, u32[]{:S(2)}) %copy-start) | copy-done | bytes 2097176
  4.9 0.0 copy-start.2
  4.9 1.6 %copy-done.2 = bf16[8,512,256]{2,1,0:T(8,128)(2,1)S(1)} copy-done((bf16[8,512,256]{2,1,0:T(8,128)(2,1)S(1)}, bf16[8,512,256]{2,1,0:T(8,128)(2,1)}, u32[]{:S(2)}) %copy-start.2) | copy-done | bytes 2097176
  6.5 0.0 copy-start.1
  6.5 0.0 copy-start.3
  6.5 0.0 copy-start.4
  6.5 0.0 copy-start.5
  6.5 34.7 %query_part.1.q_ref = bf16[128,1024]{1,0:T(8,128)(2,1)S(1)} custom-call(bf16[1,8192]{1,0:T(2,128)(2,1)S(1)} %reshape.35.gain_ref, f32[128,128]{1,0:T(8,128)S(1)} %get-tuple-element.8.cos_ref, f32[128,128]{1,0:T(8,128)S(1)} %get-tuple-element.9.sin_ref, s32[64,1]{1,0:T(8,128)S(1)} %copy.12.route_ref, s32[64,1]{1,0:T(8,128)S(1)} %copy.13.slot_ref, ...), custom_call_target="tpu_custom_call" | custom-call | tf_op jit(solution)/shard_map/query_part/pallas_call | solution.py:642
  41.3 0.0 copy-done.1
  41.3 0.0 copy-done.3
  41.3 0.0 copy-done.4
  41.3 0.0 copy-done.5
  41.3 56.8 %output_part.1 = bf16[128,8192]{1,0:T(8,128)(2,1)S(1)} custom-call(bf16[128,1024]{1,0:T(8,128)(2,1)S(1)} %query_part.1.q_ref, s32[1,192]{1,0:T(1,128)S(1)} %copy-done.3, s32[1,128]{1,0:T(1,128)S(1)} %copy-done.5, s32[1,128]{1,0:T(1,128)S(1)} %copy-done.4, s32[64,1]{1,0:T(8,128)S(1)} %copy.12.route_ref, s32[64,1]{1,0:T(8,128)S(1)} %copy.13.slot_ref, ...), custom_call_target="tpu_custom_call" | custom-call | tf_op jit(solution)/shard_map/output_part/pallas_call | solution.py:668
  98.1 1.3 %copy.17 = bf16[128,8192]{1,0:T(8,128)(2,1)} copy(bf16[128,8192]{1,0:T(8,128)(2,1)S(1)} %output_part.1) | data formatting | bytes 4194304
  (1 shorter events, 0.0 us)
Async XLA Ops:
  3.3 1.6 %copy-start = (bf16[128,8192]{1,0:T(8,128)(2,1)S(1)}, bf16[128,8192]{1,0:T(8,128)(2,1)}, u32[]{:S(2)}) copy-start(bf16[128,8192]{1,0:T(8,128)(2,1)} %hidden_hbm.3) | copy-start | bytes 6291460
  4.9 1.6 %copy-start.2 = (bf16[8,512,256]{2,1,0:T(8,128)(2,1)S(1)}, bf16[8,512,256]{2,1,0:T(8,128)(2,1)}, u32[]{:S(2)}) copy-start(bf16[8,512,256]{2,1,0:T(8,128)(2,1)} %store_hbm.3) | copy-start | bytes 6291460
  6.5 34.8 %copy-start.1 = (bf16[128,8192]{1,0:T(8,128)(2,1)S(1)}, bf16[128,8192]{1,0:T(8,128)(2,1)}, u32[]{:S(2)}) copy-start(bf16[128,8192]{1,0:T(8,128)(2,1)} %hidden_hbm.3) | copy-start | bytes 6291460
  6.5 34.8 %copy-start.3 = (s32[1,192]{1,0:T(1,128)S(1)}, s32[1,192]{1,0:T(1,128)}, u32[]{:S(2)}) copy-start(s32[1,192]{1,0:T(1,128)} %order_ref.1) | copy-start | bytes 2308
  6.5 34.8 %copy-start.4 = (s32[1,128]{1,0:T(1,128)S(1)}, s32[1,128]{1,0:T(1,128)}, u32[]{:S(2)}) copy-start(s32[1,128]{1,0:T(1,128)} %trims_ref.1) | copy-start | bytes 1540
  6.5 34.8 %copy-start.5 = (s32[1,128]{1,0:T(1,128)S(1)}, s32[1,128]{1,0:T(1,128)}, u32[]{:S(2)}) copy-start(s32[1,128]{1,0:T(1,128)} %counts_ref.1) | copy-start | bytes 1540

commit v2 on v1

v2 whole, which is shorter than its diff:
```python
import functools
import math

import jax
import jax.numpy as jnp
from jax import lax
from jax.experimental import pallas as pl
from jax.experimental.pallas import tpu as pltpu
from jax.sharding import PartitionSpec as P

MESH = pl.DeviceIdType.MESH
F32 = jnp.float32
BF16 = jnp.bfloat16

KVH = 8
HD = 128
SEG = 16
SIDE = 4
NB = 256
adapter_scale = 2.0
norm_eps = 1e-05
rope_base = 500000.0
far_score = -1e30
orders = (2, 1, 3, 0)


def iota(shape, dim):
    return lax.broadcasted_iota(jnp.int32, shape, dim)


def dot(a, b):
    return jnp.dot(a, b, preferred_element_type=F32)


def dot_nt(a, b):
    return lax.dot_general(a, b, (((1,), (1,)), ((), ())), preferred_element_type=F32)


def enter(sizes, g, t):
    groups, tensors = sizes
    barrier = pltpu.get_barrier_semaphore()

    def greet_tensor(d, c):
        pl.semaphore_signal(
            barrier, inc=1, device_id=(g, lax.rem(t + d, tensors)), device_id_type=MESH
        )
        return c

    def greet_group(d, c):
        pl.semaphore_signal(
            barrier, inc=1, device_id=(lax.rem(g + d, groups), t), device_id_type=MESH
        )
        return c

    lax.fori_loop(1, tensors, greet_tensor, 0)
    lax.fori_loop(1, groups, greet_group, 0)
    return lambda: pl.semaphore_wait(barrier, groups + tensors - 2)


def selection(route_row, slots, g, groups, cap):
    slot_rows = groups * cap * SEG
    segs = groups * 8
    value_row = slots + 1.0
    lane, sub = iota((segs, segs), 1), iota((segs, segs), 0)
    diag = lane == sub
    route_col = jnp.sum(jnp.where(diag, route_row, 0.0), axis=1, keepdims=True)
    me = g.astype(F32)
    mine = jnp.where(route_col == me, 1.0, 0.0)
    mine_row = jnp.where(route_row == me, 1.0, 0.0)
    rank = jnp.sum(
        jnp.where(((lane >> 3) == (sub >> 3)) & (lane < sub), mine_row, 0.0),
        axis=1,
        keepdims=True,
    )
    spot = mine * ((iota((segs, 1), 0) >> 3).astype(F32) * cap + rank + 1.0)
    spot_row = jnp.sum(jnp.where(diag, spot, 0.0), axis=0, keepdims=True)
    row_slot = (iota((slot_rows, segs), 0) >> 4).astype(F32) + 1.0
    adapter = jnp.sum(jnp.where(spot_row == row_slot, value_row, 0.0), axis=1, keepdims=True) - 1.0
    lane, sub = iota((segs, 128), 1), iota((segs, 128), 0)
    own_seg = lane >> 4
    in_group = (sub >> 3) == g
    r_row = jnp.sum(
        jnp.where(in_group & (own_seg == (sub & 7)), route_col, 0.0), axis=0, keepdims=True
    )
    rank = jnp.sum(
        jnp.where(in_group & (route_col == r_row) & ((sub & 7) < own_seg), 1.0, 0.0),
        axis=0,
        keepdims=True,
    )
    in_seg = (iota((1, 128), 1) & 15).astype(F32)
    spot = (r_row * cap + rank) * SEG + in_seg
    place = jnp.where(iota((slot_rows, 128), 0).astype(F32) == spot, 1.0, 0.0)
    return place, adapter


class Lora:
    def __init__(self, refs, sizes, g, t, cap):
        (
            self.xs, self.xr, self.ps, self.pr, self.ks, self.ka, self.ds, self.dr,
            self.ssem, self.rsem,
        ) = refs
        self.groups, self.tensors = sizes
        self.g, self.t, self.cap = g, t, cap
        self.rows = cap * SEG

    def pair_copy(self, src, dst, stage, peer, at):
        return pltpu.make_async_remote_copy(
            src_ref=src, dst_ref=dst,
            send_sem=self.ssem.at[stage, peer], recv_sem=self.rsem.at[stage, at],
            device_id=(peer, self.t) if stage % 2 == 0 else (self.g, peer),
            device_id_type=MESH,
        )

    def start(self, src_of, dst, stage):
        me, n = (self.g, self.groups) if stage % 2 == 0 else (self.t, self.tensors)

        def send(d, c):
            peer = lax.rem(me + d, n)
            self.pair_copy(src_of(peer), dst.at[me], stage, peer, me).start()
            return c

        lax.fori_loop(1, n, send, 0)

    def finish(self, src_of, dst, stage):
        me, n = (self.g, self.groups) if stage % 2 == 0 else (self.t, self.tensors)

        def end(d, c):
            peer = lax.rem(me + d, n)
            self.pair_copy(src_of(peer), dst.at[peer], stage, peer, peer).wait()
            return c

        lax.fori_loop(1, n, end, 0)

    def fill_rows(self, place, local):
        picked = dot(place.astype(BF16), local).astype(BF16)
        for s in range(self.groups):
            self.xs[s] = picked[s * self.rows : (s + 1) * self.rows]

    def send_rows(self):
        self.start(lambda p: self.xs.at[p], self.xr, 0)
        self.xr[self.g] = self.xs[self.g]

    def send_partials(self, adapter, store, first_lane, gain=None):
        self.finish(lambda p: self.xs.at[p], self.xr, 0)
        rows = self.xr[...].reshape(self.groups * self.rows, self.xr.shape[2])
        if gain is not None:
            rows = (rows.astype(F32) * gain).astype(BF16)
        total = jnp.zeros((self.groups * self.rows, 128), F32)
        for pair in range(4):
            factors = jnp.concatenate(
                [store[2 * pair, :, 0:128], store[2 * pair + 1, :, 0:128]], axis=1
            )
            both = dot(rows, factors)
            total = total + jnp.where(adapter == 2.0 * pair, both[:, 0:128], 0.0)
            total = total + jnp.where(adapter == 2.0 * pair + 1.0, both[:, 128:256], 0.0)
        half = total.shape[0] // 2
        low, high = total[:half], total[half:]
        if first_lane == 0:
            high = pltpu.roll(high, 64, 1)
        else:
            low = pltpu.roll(low, 64, 1)
        packed = jnp.where(iota(low.shape, 1) < 64, low, high)
        own = half // self.tensors
        for s in range(self.tensors):
            self.ps[s] = packed[s * own : (s + 1) * own]
        self.start(lambda p: self.ps.at[p], self.pr, 1)
        self.pr[self.t] = self.ps[self.t]

    def send_ranks(self):
        self.finish(lambda p: self.ps.at[p], self.pr, 1)
        total = self.pr[0]
        for s in range(1, self.tensors):
            total = total + self.pr[s]
        self.ks[...] = total.astype(BF16)
        self.start(lambda p: self.ks, self.ka, 3)
        self.ka[self.t] = self.ks[...]

    def send_updates(self, adapter, store, first_lane):
        self.finish(lambda p: self.ks, self.ka, 3)
        packed = self.ka[...].astype(F32).reshape(self.groups * self.rows // 2, 128)
        turned = pltpu.roll(packed, 64, 1)
        low, high = (packed, turned) if first_lane == 0 else (turned, packed)
        rank = jnp.concatenate([low, high], axis=0)
        lane = iota(rank.shape, 1)
        rank = jnp.where((lane >= first_lane) & (lane < first_lane + 64), rank, 0.0)
        total = None
        for pair in range(4):
            low = jnp.concatenate(
                [
                    jnp.where(adapter == 2.0 * pair, rank, 0.0),
                    jnp.where(adapter == 2.0 * pair + 1.0, rank, 0.0),
                ],
                axis=1,
            ).astype(BF16)
            factors = jnp.concatenate(
                [store[2 * pair, :, 128:256], store[2 * pair + 1, :, 128:256]], axis=1
            )
            part = dot_nt(low, factors)
            total = part if total is None else total + part
        total = total.astype(BF16)
        for s in range(self.groups):
            self.ds[s] = total[s * self.rows : (s + 1) * self.rows]
        self.start(lambda p: self.ds.at[p], self.dr, 2)
        self.dr[self.g] = self.ds[self.g]

    def update(self, place):
        self.finish(lambda p: self.ds.at[p], self.dr, 2)
        rows = self.dr[...].reshape(self.groups * self.rows, self.dr.shape[2])
        return adapter_scale * dot(place.T.astype(BF16), rows)


def lora_scratch(sizes, cap, width):
    groups, tensors = sizes
    own = groups * cap * SEG // 2 // tensors
    big = max(groups, tensors)
    return [
        pltpu.VMEM((groups, cap * SEG, width), BF16),
        pltpu.VMEM((groups, cap * SEG, width), BF16),
        pltpu.VMEM((tensors, own, 128), F32),
        pltpu.VMEM((tensors, own, 128), F32),
        pltpu.VMEM((own, 128), BF16),
        pltpu.VMEM((tensors, own, 128), BF16),
        pltpu.VMEM((groups, cap * SEG, width), BF16),
        pltpu.VMEM((groups, cap * SEG, width), BF16),
        pltpu.SemaphoreType.DMA((4, big)),
        pltpu.SemaphoreType.DMA((4, big)),
    ]


def owners(order, counts, trims, half, part, own_ref, used_ref):
    rows, pool = counts.shape[1], order.shape[1]
    square = (rows, rows)
    diag = iota(square, 0) == iota(square, 1)
    count_col = jnp.sum(jnp.where(diag, counts, 0.0), axis=1, keepdims=True)
    offsets = jnp.sum(
        jnp.where(iota(square, 0) < iota(square, 1), count_col, 0.0), axis=0, keepdims=True
    )
    lengths = counts * (2 * half) - trims
    spot = jnp.sum(
        jnp.where(
            order == iota((pool, pool), 0).astype(F32), iota((pool, pool), 1).astype(F32), 0.0
        ),
        axis=1,
        keepdims=True,
    )
    owner = (spot >= offsets) & (spot < offsets + counts)
    own_ref[...] = jnp.where(owner, 1.0, 0.0)
    first = (part * half).astype(F32)
    used = jnp.sum(
        jnp.where(owner, lengths - (spot - offsets) * (2 * half) - first, 0.0),
        axis=1,
        keepdims=True,
    )
    used_ref[...] = jnp.broadcast_to(used, (pool, 128))
    return jnp.sum(jnp.where(diag, lengths, 0.0), axis=1, keepdims=True)


def attend(own, side, q, kv_ref, half, work):
    used_ref, qp_ref, op_ref, mp_ref, lp_ref = work
    pool, rows = own.shape
    heads = q.shape[1] // HD
    block = NB // half
    used = used_ref[:, 0:1]
    qp_ref[side] = dot(own.astype(BF16), q)
    wide = (block * heads, NB)
    same_page = (iota(wide, 1) // half) == (iota(wide, 0) & (block - 1))
    slot = (iota(wide, 1) & (half - 1)).astype(F32)
    for b in range(pool // block):
        pages = slice(b * block, (b + 1) * block)
        query = jnp.concatenate(
            [qp_ref[side, pages, h * HD : (h + 1) * HD] for h in range(heads)], axis=0
        ).astype(BF16)
        keys = kv_ref[b * NB : (b + 1) * NB, 0:HD]
        values = kv_ref[b * NB : (b + 1) * NB, HD : 2 * HD]
        scores = dot_nt(query, keys) / math.sqrt(HD)
        limit = jnp.concatenate([used[pages]] * heads, axis=0)
        usable = same_page & (slot < limit)
        masked = jnp.where(usable, scores, far_score)
        top = jnp.max(masked, axis=1, keepdims=True)
        weights = jnp.where(usable, jnp.exp(masked - top), 0.0).astype(BF16)
        total = jnp.sum(weights.astype(F32), axis=1, keepdims=True)
        op_ref[side, b] = dot(weights, values)
        mp_ref[side, b] = jnp.broadcast_to(top, (block * heads, HD))
        lp_ref[side, b] = jnp.broadcast_to(total, (block * heads, HD))


def join_pages(own_ref, own_t, side, half, work, emit):
    used_ref, qp_ref, op_ref, mp_ref, lp_ref = work
    pool, rows = own_ref.shape
    block = NB // half
    heads = op_ref.shape[2] // block
    diag = iota((rows, rows), 0) == iota((rows, rows), 1)
    lane = iota((rows, HD), 1)
    summary = jnp.zeros((rows, HD), F32)
    for h in range(heads):
        inner = slice(h * block, (h + 1) * block)
        top = jnp.full((block, rows), far_score, F32)
        for b in range(pool // block):
            mine = own_ref[b * block : (b + 1) * block, :] > 0.0
            top = jnp.maximum(top, jnp.where(mine, mp_ref[side, b, inner, :], far_score))
        top = jnp.max(top, axis=0, keepdims=True)
        total = jnp.zeros((block, rows), F32)
        scaled = []
        for b in range(pool // block):
            mine = own_ref[b * block : (b + 1) * block, :] > 0.0
            page_top = jnp.max(jnp.where(mine, top, far_score), axis=1, keepdims=True)
            factor = jnp.exp(mp_ref[side, b, inner, :] - page_top)
            scaled.append(op_ref[side, b, inner, :] * factor)
            total = total + jnp.where(mine, lp_ref[side, b, inner, :] * factor, 0.0)
        total = jnp.sum(total, axis=0, keepdims=True)
        emit(h, dot(own_t, jnp.concatenate(scaled, axis=0).astype(BF16)))
        top_col = jnp.sum(jnp.where(diag, top, 0.0), axis=1, keepdims=True)
        total_col = jnp.sum(jnp.where(diag, total, 0.0), axis=1, keepdims=True)
        summary = jnp.where(lane == h, top_col, summary)
        summary = jnp.where(lane == 8 + h, total_col, summary)
    return summary


class Torus:
    def __init__(self, g, t):
        self.g, self.y, self.z = g, t // SIDE, lax.rem(t, SIDE)

    def at(self, h, da, db):
        dy, dz = (da, db) if h == 0 else (db, da)
        return lax.rem(self.y + dy, SIDE) * SIDE + lax.rem(self.z + dz, SIDE)

    def near(self, h, level, sign):
        step = 1 if sign > 0 else SIDE - 1
        return (self.g, self.at(h, step, 0) if level < 4 else self.at(h, 0, step))


def layer_kernel(
    sizes, cap,
    small_ref, gain_raw,
    hidden_hbm, matrix_hbm, store_hbm, kv_hbm, weight_hbm,
    out_ref,
    own_hidden, hidden_ref, matrix_ref, store_ref, kv_ref, weight_ref,
    gain_ref, normed_ref, inv_ref, acc_ref, q_ref,
    own_ref, used_ref, qp_ref, op_ref, mp_ref, lp_ref, o_ref, ml_ref, ms_ref,
    os_ref, or_ref, mr_ref, att_ref, snd, rcv, keep, mine, fin,
    load_sem, chunk_sem, pair_sem, rs_s, rs_r, ag_s, ag_r,
    *lora_refs,
):
    g, t = lax.axis_index("group"), lax.axis_index("tensor")
    all_in = enter(sizes, g, t)
    part = lax.rem(t, 2)
    partner = t + 1 - 2 * part
    chunks, depth, width = matrix_ref.shape
    rows, model = hidden_ref.shape
    pool = own_ref.shape[0]
    half = kv_ref.shape[0] // pool
    own_cols = pl.ds(pl.multiple_of(t * width, width), width)

    order = small_ref[:, 0:pool]
    counts = small_ref[:, 256 : 256 + rows]
    trims = small_ref[:, 384 : 384 + rows]
    segs = sizes[0] * 8
    route = small_ref[:, 512 : 512 + segs]
    slots = small_ref[:, 640 : 640 + segs]
    own_load = pltpu.make_async_copy(hidden_hbm.at[:, own_cols], own_hidden, load_sem.at[4])
    hidden_load, store_load, kv_load, weight_load = [
        pltpu.make_async_copy(src, dst, load_sem.at[i])
        for i, (src, dst) in enumerate(
            (
                (hidden_hbm, hidden_ref), (store_hbm, store_ref), (kv_hbm, kv_ref),
                (weight_hbm, weight_ref),
            )
        )
    ]
    chunk_loads = [
        pltpu.make_async_copy(
            matrix_hbm.at[pl.ds(k * depth, depth), :], matrix_ref.at[k], chunk_sem.at[k]
        )
        for k in range(chunks)
    ]
    own_load.start()
    hidden_load.start()
    chunk_loads[0].start()
    store_load.start()
    for load in chunk_loads[1:]:
        load.start()
    own_load.wait()
    place, adapter = selection(route, slots, g, sizes[0], cap)
    lora_q = Lora(lora_refs[:10], sizes, g, t, cap)
    lora = Lora(lora_refs[10:], sizes, g, t, cap)
    torus = Torus(g, t)
    lora_q.fill_rows(place, own_hidden[...])
    all_in()
    lora_q.send_rows()
    gain = gain_raw[...].astype(F32)
    for k in range(model // 128):
        gain_ref[:, k * 128 : (k + 1) * 128] = gain[k : k + 1, :]

    hidden_load.wait()

    def squares(r, c):
        at = pl.ds(pl.multiple_of(r * 16, 16), 16)
        total = jnp.zeros((16, 128), F32)
        for k in range(model // 1024):
            x = hidden_ref[at, k * 1024 : (k + 1) * 1024].astype(F32)
            x = x * x
            for j in range(8):
                total = total + x[:, j * 128 : (j + 1) * 128]
        mean = jnp.sum(total, axis=1, keepdims=True) / model
        inv = lax.rsqrt(mean + norm_eps)
        inv_ref[at, :] = jnp.broadcast_to(inv, (16, 128))
        for k in range(model // 1024):
            cols = slice(k * 1024, (k + 1) * 1024)
            normed_ref[at, cols] = (
                hidden_ref[at, cols].astype(F32) * inv * gain_ref[:, cols]
            ).astype(BF16)
        return c

    lax.fori_loop(0, rows // 16, squares, 0)

    def project(k):
        chunk_loads[k].wait()
        product = dot(normed_ref[:, k * depth : (k + 1) * depth], matrix_ref[k])
        acc_ref[...] = product if k == 0 else acc_ref[...] + product

    for k in range(chunks - 2):
        project(k)
    kv_load.start()
    weight_load.start()
    store_load.wait()
    lora_q.send_partials(adapter, store_ref, 0, gain_ref[:, own_cols])
    for k in range(chunks - 2, chunks):
        project(k)
    lengths = owners(order, counts, trims, half, part, own_ref, used_ref)
    lora_q.send_ranks()
    spin = iota((1, HD), 1) & (HD // 2 - 1)
    frequency = jnp.exp(spin.astype(F32) * (-2.0 * math.log(rope_base) / HD))
    angles = (lengths - 1.0) * frequency
    cos_table = jnp.cos(angles)
    sin_table = jnp.sin(angles) * jnp.where(iota((1, HD), 1) < HD // 2, -1.0, 1.0)
    lora_q.send_updates(adapter, store_ref, 0)
    full = acc_ref[...] + inv_ref[:, 0:1] * lora_q.update(place)
    heads = []
    for h in range(width // HD):
        x = full[:, h * HD : (h + 1) * HD]
        heads.append(x * cos_table + pltpu.roll(x, HD // 2, 1) * sin_table)
    q_ref[0] = jnp.concatenate(heads, axis=1).astype(BF16)

    def pair_copy(src, dst, i):
        return pltpu.make_async_remote_copy(
            src_ref=src, dst_ref=dst, send_sem=pair_sem.at[0, i], recv_sem=pair_sem.at[1, i],
            device_id=(g, partner), device_id_type=MESH,
        )

    query_copy = pair_copy(q_ref.at[0], q_ref.at[1], 5)
    query_copy.start()
    work = (used_ref, qp_ref, op_ref, mp_ref, lp_ref)
    own = own_ref[...]
    own_t = own.T.astype(BF16)
    kv_load.wait()
    attend(own, 0, q_ref[0], kv_ref, half, work)
    query_copy.wait()
    attend(own, 1, q_ref[1], kv_ref, half, work)
    copies = [
        pair_copy(
            os_ref.at[:, pl.ds(h * HD, HD)], or_ref.at[:, pl.ds(h * HD, HD)], h
        )
        for h in range(width // HD)
    ]

    def give(h, value):
        os_ref[:, h * HD : (h + 1) * HD] = value.astype(BF16)
        copies[h].start()

    def hold(h, value):
        o_ref[:, h * HD : (h + 1) * HD] = value

    ms_ref[...] = join_pages(own_ref, own_t, 1, half, work, give)
    summary_copy = pair_copy(ms_ref, mr_ref, 4)
    summary_copy.start()
    ml_ref[...] = join_pages(own_ref, own_t, 0, half, work, hold)
    summary_copy.wait()
    for h in range(width // HD):
        cols = slice(h * HD, (h + 1) * HD)
        own_top, other_top = ml_ref[:, h : h + 1], mr_ref[:, h : h + 1]
        top = jnp.maximum(own_top, other_top)
        own_scale, other_scale = jnp.exp(own_top - top), jnp.exp(other_top - top)
        total = ml_ref[:, 8 + h : 9 + h] * own_scale + mr_ref[:, 8 + h : 9 + h] * other_scale
        copies[h].wait()
        joined = o_ref[:, cols] * own_scale + or_ref[:, cols].astype(F32) * other_scale
        att_ref[:, cols] = (joined / total).astype(BF16)

    lora.fill_rows(place, att_ref[...])
    lora.send_rows()

    def block(h, da, db):
        col = torus.at(h, da, db) * (2 * NB) + h * NB
        return dot(att_ref[...], weight_ref[:, pl.ds(pl.multiple_of(col, NB), NB)])

    def copy_of(h, level, kind):
        return pltpu.make_async_remote_copy(
            src_ref=snd.at[h, level, kind], dst_ref=rcv.at[h, level, kind],
            send_sem=rs_s.at[h, level, kind], recv_sem=rs_r.at[h, level, kind],
            device_id=torus.near(h, level, 1 if kind % 2 == 0 else -1), device_id_type=MESH,
        )

    def send(h, level, kind, value):
        snd[h, level, kind] = value.astype(BF16)
        copy_of(h, level, kind).start()

    def got(h, level, kind):
        copy_of(h, level, kind).wait_recv()
        return rcv[h, level, kind].astype(F32)

    def send_far(h, level, value):
        send(h, level, 0, value[:64])
        send(h, level, 1, value[64:])

    def send_plus(h, level, value):
        send(h, level, 2, value[64:])
        keep[h, level, 0] = value[:64]

    def send_minus(h, level, value):
        send(h, level, 3, value[:64])
        keep[h, level, 1] = value[64:]

    def relay(h, level):
        send(h, level, 4, keep[h, level, 0] + got(h, level, 0))
        send(h, level, 5, keep[h, level, 1] + got(h, level, 1))

    def arrived(h, level, value):
        upper = value[:64] + got(h, level, 3) + got(h, level, 4)
        lower = value[64:] + got(h, level, 2) + got(h, level, 5)
        return jnp.concatenate([upper, lower], axis=0)

    weight_load.wait()
    for level, db in enumerate(orders):
        for h in range(2):
            send_far(h, level, block(h, 2, db))
    for level, db in enumerate(orders):
        for h in range(2):
            send_plus(h, level, block(h, 1, db))
            send_minus(h, level, block(h, 3, db))
    for level, db in enumerate(orders):
        for h in range(2):
            mine[h, level] = block(h, 0, db)
    lora.send_partials(adapter, store_ref, 64)
    for level in range(4):
        for h in range(2):
            relay(h, level)
    lora.send_ranks()
    for level in range(4):
        for h in range(2):
            value = arrived(h, level, mine[h, level])
            if level == 0:
                send_far(h, 4, value)
            elif level == 1:
                send_plus(h, 4, value)
            elif level == 2:
                send_minus(h, 4, value)
            else:
                fin[h] = value
    lora.send_updates(adapter, store_ref, 64)
    for h in range(2):
        relay(h, 4)
    update = lora.update(place)
    for h in range(2):
        cols = slice(h * NB, (h + 1) * NB)
        total = arrived(h, 4, fin[h]) + update[:, cols] + own_hidden[:, cols].astype(F32)
        col = t * width + h * NB
        out_ref[:, pl.ds(pl.multiple_of(col, NB), NB)] = total.astype(BF16)

    def spread(h, level, kind, da, db):
        col = torus.at(h, da, db) * (2 * NB) + h * NB
        upper = kind in (0, 3, 4)
        half_rows = out_ref.shape[0] // 2
        rows = slice(0, half_rows) if upper else slice(half_rows, 2 * half_rows)
        place_at = out_ref.at[rows, pl.ds(pl.multiple_of(col, NB), NB)]
        return pltpu.make_async_remote_copy(
            src_ref=place_at, dst_ref=place_at,
            send_sem=ag_s.at[h, level, kind], recv_sem=ag_r.at[h, level, kind],
            device_id=torus.near(h, level, 1 if kind % 2 == 0 else -1), device_id_type=MESH,
        )

    sent = (0, 0, 0, 0, 3, 1)
    brought = (3, 1, 3, 1, 2, 2)

    def go(h, level, kind):
        if level == 4:
            spread(h, level, kind, 0, sent[kind]).start()
        else:
            spread(h, level, kind, sent[kind], level).start()

    def came(h, level, kind):
        if level == 4:
            spread(h, level, kind, 0, brought[kind]).wait_recv()
        else:
            spread(h, level, kind, brought[kind], level).wait_recv()

    def left(h, level, kind):
        if level == 4:
            spread(h, level, kind, 0, sent[kind]).wait_send()
        else:
            spread(h, level, kind, sent[kind], level).wait_send()

    def go_all(h, level, kinds):
        for kind in kinds:
            go(h, level, kind)

    def pass_on(h, level):
        came(h, level, 0)
        go(h, level, 4)
        came(h, level, 1)
        go(h, level, 5)

    for level in (4, 0):
        for h in range(2):
            go_all(h, level, range(4))
    for h in range(2):
        pass_on(h, 4)
        go_all(h, 3, (0, 3))
        go_all(h, 1, (1, 2))
    for h in range(2):
        came(h, 4, 2)
        go_all(h, 3, (2, 1))
        came(h, 4, 3)
        go_all(h, 1, (0, 3))
    for h in range(2):
        pass_on(h, 0)
    for h in range(2):
        came(h, 4, 4)
        go_all(h, 2, (0, 3))
        came(h, 4, 5)
        go_all(h, 2, (1, 2))
    for level in (3, 1, 2):
        for h in range(2):
            pass_on(h, level)
    for level in (0, 3, 1, 2):
        for h in range(2):
            for kind in range(2, 6):
                came(h, level, kind)
    for level in range(5):
        for h in range(2):
            for kind in range(6):
                copy_of(h, level, kind).wait_send()
                left(h, level, kind)


def body(
    sizes,
    hidden, norm_gain, query_matrix, output_weight, kv_pages, page_order, page_counts,
    page_trims, adapter_store, store_route, store_slot,
):
    groups = sizes[0]
    cap = max(2, 16 // groups) if groups > 1 else 8
    rows, width = hidden.shape
    local_width = query_matrix.shape[1]
    pool, _, half, lanes = kv_pages.shape
    stored = adapter_store.shape[0]
    hbm = pl.BlockSpec(memory_space=pltpu.HBM)
    vmem = pl.BlockSpec(memory_space=pltpu.VMEM)

    def at_lane(value, first):
        row = value.reshape(1, -1)
        return jnp.pad(row, ((0, 0), (first, 768 - first - row.shape[1])))

    small = (
        at_lane(page_order, 0) + at_lane(page_counts, 256) + at_lane(page_trims, 384)
        + at_lane(store_route, 512) + at_lane(store_slot, 640)
    ).astype(F32)
    chunks = 8
    blocks = pool * half // NB
    block_rows = (NB // half) * (local_width // HD)
    return pl.pallas_call(
        functools.partial(layer_kernel, sizes, cap),
        out_shape=jax.ShapeDtypeStruct((rows, width), BF16),
        in_specs=[vmem] * 2 + [hbm] * 5,
        out_specs=vmem,
        scratch_shapes=[
            pltpu.VMEM((rows, local_width), BF16),
            pltpu.VMEM((rows, width), BF16),
            pltpu.VMEM((chunks, width // chunks, local_width), BF16),
            pltpu.VMEM((stored, local_width, lanes), BF16),
            pltpu.VMEM((pool * half, lanes), BF16),
            pltpu.VMEM((local_width, width), BF16),
            pltpu.VMEM((1, width), F32),
            pltpu.VMEM((rows, width), BF16),
            pltpu.VMEM((rows, 128), F32),
            pltpu.VMEM((rows, local_width), F32),
            pltpu.VMEM((2, rows, local_width), BF16),
            pltpu.VMEM((pool, rows), F32),
            pltpu.VMEM((pool, 128), F32),
            pltpu.VMEM((2, pool, local_width), F32),
            pltpu.VMEM((2, blocks, block_rows, HD), F32),
            pltpu.VMEM((2, blocks, block_rows, HD), F32),
            pltpu.VMEM((2, blocks, block_rows, HD), F32),
            pltpu.VMEM((rows, local_width), F32),
            pltpu.VMEM((rows, 128), F32),
            pltpu.VMEM((rows, 128), F32),
            pltpu.VMEM((rows, local_width), BF16),
            pltpu.VMEM((rows, local_width), BF16),
            pltpu.VMEM((rows, 128), F32),
            pltpu.VMEM((rows, local_width), BF16),
            pltpu.VMEM((2, 5, 6, rows // 2, NB), BF16),
            pltpu.VMEM((2, 5, 6, rows // 2, NB), BF16),
            pltpu.VMEM((2, 5, 2, rows // 2, NB), F32),
            pltpu.VMEM((2, 4, rows, NB), F32),
            pltpu.VMEM((2, rows, NB), F32),
            pltpu.SemaphoreType.DMA((5,)),
            pltpu.SemaphoreType.DMA((chunks,)),
            pltpu.SemaphoreType.DMA((2, 6)),
            pltpu.SemaphoreType.DMA((2, 5, 6)),
            pltpu.SemaphoreType.DMA((2, 5, 6)),
            pltpu.SemaphoreType.DMA((2, 5, 6)),
            pltpu.SemaphoreType.DMA((2, 5, 6)),
        ]
        + lora_scratch(sizes, cap, local_width)
        + lora_scratch(sizes, cap, local_width),
        compiler_params=pltpu.CompilerParams(
            collective_id=0, has_side_effects=True, vmem_limit_bytes=50 << 20
        ),
        name="layer",
    )(
        small, norm_gain.reshape(width // 128, 128), hidden, query_matrix, adapter_store, kv_pages.reshape(pool * half, lanes), output_weight,
    )


def solution(mesh):
    sizes = (mesh.shape["group"], mesh.shape["tensor"])
    in_specs = (
        P("group", None),
        P(),
        P(None, "tensor"),
        P("tensor", None),
        P("group", "tensor", None, None),
        P("group", None),
        P("group", None),
        P("group", None),
        P("group", "tensor", None),
        P(),
        P(),
    )
    return jax.shard_map(
        functools.partial(body, sizes),
        mesh=mesh,
        in_specs=in_specs,
        out_specs=P("group", None),
        check_vma=False,
    )
```

time: 99.7 us -> 91.5 us (0.918)
  local copies, waits for them, and re-layouts: 6.74 us -> 2.04 us
  Pallas kernels: 91.5 us -> 88.5 us
    unnamed x14 -> x3, local copies, waits for them, and re-layouts: 5.26 us -> 2.04 us
    pallas_call x2 -> x1, Pallas kernels: 91.5 us -> 88.5 us  [body(): pl.pallas_call(functools.partial(layer_kernel, sizes, cap), out_shape=jax...]
    reshape x2 -> x0, local copies, waits for them, and re-layouts: 1.48 us -> none  [the longest x1 0.74 us: body(): slots = store_slot.reshape(-1, 1)]
where the time goes in v2:
time: 91.5 us; the launch traced here: 91.3 us
  Pallas kernels  88.5 us (97%)
  local copies, waits for them, and re-layouts  2.04 us (2%)
    pallas_call x1, Pallas kernels, body(): pl.pallas_call(functools.partial(layer_kernel, sizes, cap), out_shape=jax...  88.5 us
    unnamed x3, local copies, waits for them, and re-layouts  2.04 us

profile of v2, /device:TPU:0, one launch (start us, length us, event | category | flops | bytes accessed | tf_op | source)
XLA Modules:
  0.0 91.3 jit_solution(3298108774865886484)
XLA Ops:
  0.0 0.7 add_convert_fusion.small_ref
  0.8 0.0 copy-start
  0.8 0.7 copy-done
  1.5 88.5 %layer.1 = bf16[128,8192]{1,0:T(8,128)(2,1)S(1)} custom-call(f32[1,768]{1,0:T(1,128)S(1)} %add_convert_fusion.small_ref, bf16[64,128]{1,0:T(8,128)(2,1)S(1)} %bitcast.4, bf16[128,8192]{1,0:T(8,128)(2,1)} %hidden_hbm.1, bf16[8192,512]{1,0:T(8,128)(2,1)} %matrix_hbm.1, bf16[8,512,256]{2,1,0:T(8,128)(2,1)} %store_hbm.1, bf16[6144,256]{1,0:T(8,128)(2,1)} %bitcast.5, ...), custom_call_target="tpu_custom_call" | custom-call | tf_op jit(solution)/shard_map/layer/pallas_call | solution.py:669
  90.0 1.3 %copy.13 = bf16[128,8192]{1,0:T(8,128)(2,1)} copy(bf16[128,8192]{1,0:T(8,128)(2,1)S(1)} %layer.1) | data formatting | bytes 4194304
Async XLA Ops:
  0.8 0.7 copy-start

commit v3 on v2

--- a/solution.py
+++ b/solution.py
@@ -209,6 +209,82 @@
         return adapter_scale * dot(place.T.astype(BF16), rows)
 
 
+    def send_group_partials(self, rows, spot, factors):
+        lane_half = iota((rows.shape[0], 128), 1) >> 6
+        total = jnp.zeros((rows.shape[0], 128), F32)
+        for pair in range(self.groups // 2):
+            both = dot(rows, jnp.concatenate([factors[2 * pair], factors[2 * pair + 1]], axis=1))
+            for i in range(2):
+                mine = (spot - 2 * (2 * pair + i)) == lane_half
+                total = total + jnp.where(mine, both[:, i * 128 : (i + 1) * 128], 0.0)
+        own = total.shape[0] // self.tensors
+        for s in range(self.tensors):
+            self.ps[s] = total[s * own : (s + 1) * own]
+        self.start(lambda p: self.ps.at[p], self.pr, 1)
+        self.pr[self.t] = self.ps[self.t]
+
+    def group_update(self, spot, factors):
+        rank = self.ka[...].astype(F32).reshape(-1, 128)
+        store = spot >> 1
+        total = None
+        for pair in range(self.groups // 2):
+            low = jnp.concatenate(
+                [jnp.where(store == 2 * pair + i, rank, 0.0) for i in range(2)], axis=1
+            ).astype(BF16)
+            up = jnp.concatenate([factors[2 * pair], factors[2 * pair + 1]], axis=1)
+            part = dot_nt(low, up)
+            total = part if total is None else total + part
+        return adapter_scale * total
+
+
+class Factors:
+    def __init__(self, sems, g, t, groups):
+        self.ssem, self.rsem = sems
+        self.g, self.t, self.groups = g, t, groups
+
+    def double(self, store, first, twice):
+        row, col = iota((128, 128), 0), iota((128, 128), 1)
+        repeat = jnp.where(row == 64 + (col & 63), 1.0, 0.0).astype(BF16)
+        for a in range(store.shape[0]):
+            twice[a] = dot(store[a, :, first : first + 128], repeat).astype(BF16)
+
+    def choose(self, twice, adapter, out, held):
+        lane = iota((1, 128), 1)
+        for s in range(self.groups):
+            left_one = adapter[2 * s * SEG : 2 * s * SEG + 1, :]
+            right_one = adapter[(2 * s + 1) * SEG : (2 * s + 1) * SEG + 1, :]
+            named = jnp.where(lane < 64, left_one, right_one)
+            total = None
+            for a in range(twice.shape[0]):
+                part = twice[a] * jnp.where(named == 1.0 * a, 1.0, 0.0).astype(BF16)
+                total = part if total is None else total + part
+            out[s] = total
+        held[self.g] = out[self.g]
+
+    def copy(self, out, held, kind, rows, peer, at):
+        return pltpu.make_async_remote_copy(
+            src_ref=out.at[peer, rows], dst_ref=held.at[at, rows],
+            send_sem=self.ssem.at[kind, peer], recv_sem=self.rsem.at[kind, at],
+            device_id=(peer, self.t), device_id_type=MESH,
+        )
+
+    def start(self, out, held, kind, rows):
+        def send(d, c):
+            peer = lax.rem(self.g + d, self.groups)
+            self.copy(out, held, kind, rows, peer, self.g).start()
+            return c
+
+        lax.fori_loop(1, self.groups, send, 0)
+
+    def finish(self, out, held, kind, rows):
+        def end(d, c):
+            peer = lax.rem(self.g + d, self.groups)
+            self.copy(out, held, kind, rows, peer, peer).wait()
+            return c
+
+        lax.fori_loop(1, self.groups, end, 0)
+
+
 def lora_scratch(sizes, cap, width):
     groups, tensors = sizes
     own = groups * cap * SEG // 2 // tensors
@@ -338,7 +414,7 @@
     gain_ref, normed_ref, inv_ref, acc_ref, q_ref,
     own_ref, used_ref, qp_ref, op_ref, mp_ref, lp_ref, o_ref, ml_ref, ms_ref,
     os_ref, or_ref, mr_ref, att_ref, snd, rcv, keep, mine, fin,
-    load_sem, chunk_sem, pair_sem, rs_s, rs_r, ag_s, ag_r,
+    load_sem, chunk_sem, pair_sem, twice, down_s, down_r, up_s, up_r, fac_s, fac_r, rs_s, rs_r, ag_s, ag_r,
     *lora_refs,
 ):
     g, t = lax.axis_index("group"), lax.axis_index("tensor")
@@ -382,7 +458,13 @@
     own_load.wait()
     place, adapter = selection(route, slots, g, sizes[0], cap)
     lora_q = Lora(lora_refs[:10], sizes, g, t, cap)
-    lora = Lora(lora_refs[10:], sizes, g, t, cap)
+    lora = Lora((None, None, *lora_refs[10:14], None, None, *lora_refs[14:]), sizes, g, t, cap)
+    factors = Factors((fac_s, fac_r), g, t, sizes[0])
+    first_rows, last_rows, all_rows = pl.ds(0, 192), pl.ds(192, width - 192), pl.ds(0, width)
+    place_t = place.T
+    spot = jnp.sum(
+        jnp.where(place_t > 0.0, (iota(place_t.shape, 1) >> 4).astype(F32), 0.0), axis=1, keepdims=True
+    ).astype(jnp.int32)
     torus = Torus(g, t)
     lora_q.fill_rows(place, own_hidden[...])
     all_in()
@@ -423,7 +505,10 @@
     kv_load.start()
     weight_load.start()
     store_load.wait()
+    factors.double(store_ref, 0, twice)
     lora_q.send_partials(adapter, store_ref, 0, gain_ref[:, own_cols])
+    factors.choose(twice, adapter, down_s, down_r)
+    factors.start(down_s, down_r, 0, first_rows)
     for k in range(chunks - 2, chunks):
         project(k)
     lengths = owners(order, counts, trims, half, part, own_ref, used_ref)
@@ -434,6 +519,10 @@
     cos_table = jnp.cos(angles)
     sin_table = jnp.sin(angles) * jnp.where(iota((1, HD), 1) < HD // 2, -1.0, 1.0)
     lora_q.send_updates(adapter, store_ref, 0)
+    factors.start(down_s, down_r, 1, last_rows)
+    factors.double(store_ref, 128, twice)
+    factors.choose(twice, adapter, up_s, up_r)
+    factors.start(up_s, up_r, 2, all_rows)
     full = acc_ref[...] + inv_ref[:, 0:1] * lora_q.update(place)
     heads = []
     for h in range(width // HD):
@@ -485,8 +574,6 @@
         joined = o_ref[:, cols] * own_scale + or_ref[:, cols].astype(F32) * other_scale
         att_ref[:, cols] = (joined / total).astype(BF16)
 
-    lora.fill_rows(place, att_ref[...])
-    lora.send_rows()
 
     def block(h, da, db):
         col = torus.at(h, da, db) * (2 * NB) + h * NB
@@ -532,6 +619,9 @@
     for level, db in enumerate(orders):
         for h in range(2):
             send_far(h, level, block(h, 2, db))
+    factors.finish(down_s, down_r, 0, first_rows)
+    factors.finish(down_s, down_r, 1, last_rows)
+    lora.send_group_partials(att_ref[...], spot, down_r)
     for level, db in enumerate(orders):
         for h in range(2):
             send_plus(h, level, block(h, 1, db))
@@ -539,7 +629,6 @@
     for level, db in enumerate(orders):
         for h in range(2):
             mine[h, level] = block(h, 0, db)
-    lora.send_partials(adapter, store_ref, 64)
     for level in range(4):
         for h in range(2):
             relay(h, level)
@@ -555,10 +644,11 @@
                 send_minus(h, 4, value)
             else:
                 fin[h] = value
-    lora.send_updates(adapter, store_ref, 64)
     for h in range(2):
         relay(h, 4)
-    update = lora.update(place)
+    lora.finish(lambda p: lora.ks, lora.ka, 3)
+    factors.finish(up_s, up_r, 2, all_rows)
+    update = lora.group_update(spot, up_r)
     for h in range(2):
         cols = slice(h * NB, (h + 1) * NB)
         total = arrived(h, 4, fin[h]) + update[:, cols] + own_hidden[:, cols].astype(F32)
@@ -704,13 +794,20 @@
             pltpu.SemaphoreType.DMA((5,)),
             pltpu.SemaphoreType.DMA((chunks,)),
             pltpu.SemaphoreType.DMA((2, 6)),
+            pltpu.VMEM((stored, local_width, 128), BF16),
+            pltpu.VMEM((groups, local_width, 128), BF16),
+            pltpu.VMEM((groups, local_width, 128), BF16),
+            pltpu.VMEM((groups, local_width, 128), BF16),
+            pltpu.VMEM((groups, local_width, 128), BF16),
+            pltpu.SemaphoreType.DMA((3, groups)),
+            pltpu.SemaphoreType.DMA((3, groups)),
             pltpu.SemaphoreType.DMA((2, 5, 6)),
             pltpu.SemaphoreType.DMA((2, 5, 6)),
             pltpu.SemaphoreType.DMA((2, 5, 6)),
             pltpu.SemaphoreType.DMA((2, 5, 6)),
         ]
         + lora_scratch(sizes, cap, local_width)
-        + lora_scratch(sizes, cap, local_width),
+        + [x for i, x in enumerate(lora_scratch(sizes, cap, local_width)) if i not in (0, 1, 6, 7)],
         compiler_params=pltpu.CompilerParams(
             collective_id=0, has_side_effects=True, vmem_limit_bytes=50 << 20
         ),

time: 91.5 us -> 88.4 us (0.966)
  Pallas kernels: 88.5 us -> 85.4 us
    pallas_call x1, Pallas kernels: 88.5 us -> 85.4 us  [body(): pl.pallas_call(functools.partial(layer_kernel, sizes, cap), out_shape=jax...]
where the time goes in v3:
time: 88.4 us; the launch traced here: 88.2 us
  Pallas kernels  85.4 us (97%)
  local copies, waits for them, and re-layouts  2.04 us (2%)
    pallas_call x1, Pallas kernels, body(): pl.pallas_call(functools.partial(layer_kernel, sizes, cap), out_shape=jax...  85.4 us
    unnamed x3, local copies, waits for them, and re-layouts  2.04 us

profile of v3, /device:TPU:0, one launch (start us, length us, event | category | flops | bytes accessed | tf_op | source)
XLA Modules:
  0.0 88.2 jit_solution(15114025724365375196)
XLA Ops:
  0.0 0.7 add_convert_fusion.small_ref
  0.8 0.0 copy-start
  0.8 0.7 copy-done
  1.5 85.4 %layer.1 = bf16[128,8192]{1,0:T(8,128)(2,1)S(1)} custom-call(f32[1,768]{1,0:T(1,128)S(1)} %add_convert_fusion.small_ref, bf16[64,128]{1,0:T(8,128)(2,1)S(1)} %bitcast.4, bf16[128,8192]{1,0:T(8,128)(2,1)} %hidden_hbm.1, bf16[8192,512]{1,0:T(8,128)(2,1)} %matrix_hbm.1, bf16[8,512,256]{2,1,0:T(8,128)(2,1)} %store_hbm.1, bf16[6144,256]{1,0:T(8,128)(2,1)} %bitcast.5, ...), custom_call_target="tpu_custom_call" | custom-call | tf_op jit(solution)/shard_map/layer/pallas_call | solution.py:759
  86.8 1.3 %copy.13 = bf16[128,8192]{1,0:T(8,128)(2,1)} copy(bf16[128,8192]{1,0:T(8,128)(2,1)S(1)} %layer.1) | data formatting | bytes 4194304
Async XLA Ops:
  0.8 0.7 copy-start
